TPU v7x, 128 devices: a whole 4x4x4 slice. The times are simulated.
128 devices in a mesh: omega: 16 (over x, z_hi, core), row: 8 (over y, z_lo).
Axes of the slice: x: 4, y: 4, z: 4 (z_hi: 2, z_lo: 2; z = z_hi * 2 + z_lo), core: 2. Of those that a mesh axis runs over, the one named last changes fastest.
Arguments:
- frames: float32 [256, 512, 1024], P('omega', 'row'), may hold values from -6 to 6
- thresholds: int32 [512], P('row'), may hold values from 0 to 31
- spot_boxes: int32 [3, 4096], P(None, ('omega', 'row')), may hold values from -1 to 1023, as said below
Outputs:
- peak_weight: float32 [256, 512, 1024], P('omega', 'row')
- moments: float32 [4, 4096], P(None, ('omega', 'row'))
Inputs may be any that keep to these rules, and one draw needn't show every extreme that they name: `spot_boxes`: slot block d of 32 slots (d = omega index * the number of row indices + row index) lists boxes that lie wholly inside the frames and rows of that device; its live boxes fill the leading slots, each block has 1 to 32 of them, and one block has 32; empty slots hold -1 in all three entries.
All inputs are finite; a program needn't handle non-finite values.
Results may differ from a plain program's by a relative error of at most 0.0003.
Values sent between devices are 32-bit elements; how exact they have to be, the bound alone decides.
A program may use at most 64 MiB of HBM per device.

v0:
```python
import jax
import jax.numpy as jnp
from jax import lax
from jax.sharding import PartitionSpec as P

BW = 4
BOX_F = 8
BOX_R = 16
BOX_C = 16


SHARP = 8.0


def extended_2(x, sides, width, wrap):
    for axis, dim in sides:
        peers, length = (lax.axis_size(axis), x.shape[dim])
        up = [(i, (i + 1) % peers) for i in range(peers if wrap else peers - 1)]
        down = [(j, i) for i, j in up]
        last = lax.slice_in_dim(x, length - width, length, axis=dim)
        leading = lax.slice_in_dim(x, 0, width, axis=dim)
        before = lax.ppermute(last, axis, up)
        after = lax.ppermute(leading, axis, down)
        x = jnp.concatenate([before, x, after], axis=dim)
    return x


def selectors(start, length, extent, live):
    places = jnp.arange(extent)
    distance = places[None, :] - start[:, None]
    inside = (distance >= 0) & (distance < length) & live[:, None]
    middle = (length - 1) / 2.0
    offset = (distance.astype(jnp.float32) - middle) / middle
    member = jnp.where(inside, 1.0, 0.0).astype(jnp.float32)
    return (member, member * offset)


def frame_filter(padded):
    return (padded[:-2] + 2.0 * padded[1:-1] + padded[2:]) * 0.25


def row_filter(padded):
    return (padded[:, :-2] + 2.0 * padded[:, 1:-1] + padded[:, 2:]) * 0.25


def column_filter(values):
    padded = jnp.pad(values, ((0, 0), (0, 0), (1, 1)))
    return (padded[:, :, :-2] + 2.0 * padded[:, :, 1:-1] + padded[:, :, 2:]) * 0.25


def frame_maxima(padded):
    return jnp.maximum(jnp.maximum(padded[:-2], padded[1:-1]), padded[2:])


def row_maxima(padded):
    position = lax.axis_index("row")
    final = lax.axis_size("row") - 1
    upper = jnp.where(position == 0, padded[:, 1:2], padded[:, 0:1])
    lower = jnp.where(position == final, padded[:, -2:-1], padded[:, -1:])
    fixed = jnp.concatenate([upper, padded[:, 1:-1], lower], axis=1)
    return jnp.maximum(jnp.maximum(fixed[:, :-2], fixed[:, 1:-1]), fixed[:, 2:])


def column_maxima(values):
    padded = jnp.pad(values, ((0, 0), (0, 0), (1, 1)), mode="edge")
    return jnp.maximum(jnp.maximum(padded[:, :, :-2], padded[:, :, 1:-1]), padded[:, :, 2:])


def on_device(frames, thresholds, spot_boxes):
    frame_count = frames.shape[0]
    row_count = frames.shape[1]
    column_count = frames.shape[2]
    span = 2 * BW + 1
    extended = extended_2(frames, (("omega", 0),), BW, True)
    total = extended[0:frame_count]
    for offset in range(1, span):
        total = total + extended[offset : offset + frame_count]
    corrected = frames - total / span
    padded = extended_2(corrected, (("omega", 0),), 1, True)
    smooth = frame_filter(padded)
    padded = extended_2(smooth, (("row", 1),), 1, False)
    smooth = column_filter(row_filter(padded))
    padded = extended_2(smooth, (("omega", 0),), 1, True)
    highest = frame_maxima(padded)
    padded = extended_2(highest, (("row", 1),), 1, False)
    highest = column_maxima(row_maxima(padded))
    level = thresholds.astype(jnp.float32) / 64.0
    weight = jnp.exp(SHARP * (smooth - highest)) * jnp.maximum(smooth - level[None, :, None], 0.0)
    frame_base = lax.axis_index("omega") * frame_count
    row_base = lax.axis_index("row") * row_count
    live = spot_boxes[0] >= 0
    slots = spot_boxes.shape[1]
    frame_pick, frame_moment = selectors(spot_boxes[0] - frame_base, BOX_F, frame_count, live)
    row_pick, row_moment = selectors(spot_boxes[1] - row_base, BOX_R, row_count, live)
    column_pick, column_moment = selectors(spot_boxes[2], BOX_C, column_count, live)
    stacked = jnp.concatenate([column_pick, column_moment], axis=0)
    folded = jnp.einsum("frc,kc->kfr", weight, stacked, precision=lax.Precision.HIGHEST)
    plain = folded[:slots]
    by_column = folded[slots:]
    plain_rows = jnp.sum(plain * row_pick[:, None, :], axis=2)
    moment_rows = jnp.sum(plain * row_moment[:, None, :], axis=2)
    column_rows = jnp.sum(by_column * row_pick[:, None, :], axis=2)
    stats = jnp.stack(
        [
            jnp.sum(plain_rows * frame_pick, axis=1),
            jnp.sum(plain_rows * frame_moment, axis=1),
            jnp.sum(moment_rows * frame_pick, axis=1),
            jnp.sum(column_rows * frame_pick, axis=1),
        ]
    )
    return (weight, stats / float(BOX_F * BOX_R * BOX_C))


def solution(mesh):
    return jax.shard_map(
        on_device,
        mesh=mesh,
        in_specs=(P("omega", "row", None), P("row"), P(None, ("omega", "row"))),
        out_specs=(P("omega", "row", None), P(None, ("omega", "row"))),
        check_vma=False,
    )
```

profile of v0, /device:TPU:1, one launch (start us, length us, event | category | flops | bytes accessed | tf_op | source)
XLA Modules:
  0.0 116.8 jit_solution(138033203455745731)
XLA Ops:
  0.6 0.0 copy-start.5
  0.6 1.8 %fusion.49 = (f32[4,64,1024]{2,1,0:T(8,128)S(1)}, f32[4,64,1024]{2,1,0:T(8,128)S(1)}) fusion(f32[16,64,1024]{2,1,0:T(8,128)} %param.3), kind=kLoop, calls=%fused_computation.95 | loop fusion | bytes 4194304 | tf_op jit(solution)/shard_map/slice | solution.py:20
  2.5 5.0 %collective-permute-start = (f32[4,64,1024]{2,1,0:T(8,128)S(1)}, f32[4,64,1024]{2,1,0:T(8,128)S(1)}, u32[]{:S(2)}, u32[]{:S(2)}) collective-permute-start(f32[4,64,1024]{2,1,0:T(8,128)S(1)} %get-tuple-element.23), channel_id=1, source_target_pairs={{0,8},{8,16},{16,24},{24,32},{32,40},{40,48},{48,56},{56,64},{64,7... | collective-permute-start | bytes 3145736 | tf_op jit(solution)/shard_map/ppermute | solution.py:22
  7.5 0.0 collective-permute-start.1
  7.5 23.0 %collective-permute-done = f32[4,64,1024]{2,1,0:T(8,128)S(1)} collective-permute-done((f32[4,64,1024]{2,1,0:T(8,128)S(1)}, f32[4,64,1024]{2,1,0:T(8,128)S(1)}, u32[]{:S(2)}, u32[]{:S(2)}) %collective-permute-start) | collective-permute-done | bytes 1048608 | tf_op jit(solution)/shard_map/ppermute | solution.py:22
  30.5 0.1 constant_dynamic-update-slice_fusion.1
  30.6 0.0 copy-done.5
  30.6 0.9 constant_dynamic-update-slice_fusion
  31.5 0.0 copy-start.2
  31.5 1.1 collective-permute-done.1
  32.6 0.1 constant_dynamic-update-slice_fusion.2
  32.6 1.1 copy-done.2
  33.8 0.0 copy-start.8
  33.8 8.7 %fusion.18 = f32[16,64,1024]{2,1,0:T(8,128)S(1)} fusion(f32[16,64,1024]{2,1,0:T(8,128)S(1)} %copy-done.5, f32[20,64,1024]{2,1,0:T(8,128)S(1)} %constant_dynamic-update-slice_fusion.2, f32[20,64,1024]{2,1,0:T(8,128)} %copy-done.2), kind=kLoop, calls=%fused_computation.31 | loop fusion | flops 10485760 | bytes 41943040 | tf_op jit(solution)/shard_map/sub | solution.py:78
  42.5 0.0 copy-start
  42.5 2.0 %copy-done = f32[16,64,1024]{2,1,0:T(8,128)} copy-done((f32[16,64,1024]{2,1,0:T(8,128)}, f32[16,64,1024]{2,1,0:T(8,128)S(1)}, u32[]{:S(2)}) %copy-start) | copy-done | bytes 4194328
  44.5 4.1 %collective-permute-start.2 = (f32[1,64,1024]{2,1,0:T(8,128)S(1)}, f32[1,64,1024]{2,1,0:T(8,128)S(1)}, u32[]{:S(2)}, u32[]{:S(2)}) collective-permute-start(f32[1,64,1024]{2,1,0:T(8,128)S(1)} %get-tuple-element.19), channel_id=1, source_target_pairs={{0,8},{8,16},{16,24},{24,32},{32,40},{40,48},{48,56},{56,64},{64,7... | collective-permute-start | bytes 786440 | tf_op jit(solution)/shard_map/ppermute | solution.py:22
  48.6 0.0 collective-permute-start.3
  48.6 0.0 copy-done.8
  48.6 0.0 copy-start.1
  48.6 3.7 %collective-permute-done.2 = f32[1,64,1024]{2,1,0:T(8,128)S(1)} collective-permute-done((f32[1,64,1024]{2,1,0:T(8,128)S(1)}, f32[1,64,1024]{2,1,0:T(8,128)S(1)}, u32[]{:S(2)}, u32[]{:S(2)}) %collective-permute-start.2) | collective-permute-done | bytes 262176 | tf_op jit(solution)/shard_map/ppermute | solution.py:22
  52.3 3.5 %collective-permute-done.3 = f32[1,64,1024]{2,1,0:T(8,128)S(1)} collective-permute-done((f32[1,64,1024]{2,1,0:T(8,128)S(1)}, f32[1,64,1024]{2,1,0:T(8,128)S(1)}, u32[]{:S(2)}, u32[]{:S(2)}) %collective-permute-start.3) | collective-permute-done | bytes 262176 | tf_op jit(solution)/shard_map/ppermute | solution.py:23
  55.9 5.6 %broadcast_multiply_fusion.1 = f32[16,64,1024]{2,1,0:T(8,128)S(1)} fusion(f32[1,64,1024]{2,1,0:T(8,128)S(1)} %collective-permute-done.3, f32[16,64,1024]{2,1,0:T(8,128)} %copy-done, f32[1,64,1024]{2,1,0:T(8,128)S(1)} %collective-permute-done.2), kind=kLoop, calls=%fused_computation.40 | loop fusion | flops 6291456 | bytes 8912896 | tf_op jit(solution)/shard_map/mul | solution.py:39
  61.5 0.1 fusion.47
  61.6 2.6 %collective-permute-start.4 = (f32[16,1,1024]{2,1,0:T(1,128)S(1)}, f32[16,1,1024]{2,1,0:T(1,128)S(1)}, u32[]{:S(2)}, u32[]{:S(2)}) collective-permute-start(f32[16,1,1024]{2,1,0:T(1,128)S(1)} %get-tuple-element.17), channel_id=1, source_target_pairs={{0,1},{1,2},{2,3},{3,4},{4,5},{5,6},{6,7},{8,9},{9,10},{10,11},{11... | collective-permute-start | bytes 196616 | tf_op jit(solution)/shard_map/ppermute | solution.py:22
  64.3 1.3 %collective-permute-start.5 = (f32[16,1,1024]{2,1,0:T(1,128)S(1)}, f32[16,1,1024]{2,1,0:T(1,128)S(1)}, u32[]{:S(2)}, u32[]{:S(2)}) collective-permute-start(f32[16,1,1024]{2,1,0:T(1,128)S(1)} %get-tuple-element.18), channel_id=1, source_target_pairs={{1,0},{2,1},{3,2},{4,3},{5,4},{6,5},{7,6},{9,8},{10,9},{11,10},{12... | collective-permute-start | bytes 196616 | tf_op jit(solution)/shard_map/ppermute | solution.py:23
  65.6 0.1 collective-permute-done.4
  65.7 3.9 %collective-permute-done.5 = f32[16,1,1024]{2,1,0:T(1,128)S(1)} collective-permute-done((f32[16,1,1024]{2,1,0:T(1,128)S(1)}, f32[16,1,1024]{2,1,0:T(1,128)S(1)}, u32[]{:S(2)}, u32[]{:S(2)}) %collective-permute-start.5) | collective-permute-done | bytes 65568 | tf_op jit(solution)/shard_map/ppermute | solution.py:23
  69.6 0.0 copy-done.1
  69.6 3.1 %broadcast_multiply_fusion = f32[16,64,1024]{2,1,0:T(8,128)S(1)} fusion(f32[16,1,1024]{2,1,0:T(1,128)S(1)} %collective-permute-done.5, f32[16,64,1024]{2,1,0:T(8,128)S(1)} %broadcast_multiply_fusion.1, f32[1,64,1024]{2,1,0:T(8,128)S(1)} %collective-permute-done.3, f32[16,64,1024]{2,1,0:T(8,128)S(1)} %copy-done.1, ...), kind=kLoop, calls=%fused_computation.39 | loop fusion | flops 11534336 | bytes 13238272 | tf_op jit(solution)/shard_map/mul | solution.py:43
  72.7 4.6 %fusion.2 = f32[16,64,1024]{2,1,0:T(8,128)S(1)} fusion(f32[16,64,1024]{2,1,0:T(8,128)S(1)} %broadcast_multiply_fusion, f32[16,1,1024]{2,1,0:T(1,128)S(1)} %collective-permute-done.5, f32[16,64,1024]{2,1,0:T(8,128)S(1)} %broadcast_multiply_fusion.1, f32[1,64,1024]{2,1,0:T(8,128)S(1)} %collective-permute-done.3, f32[16,64,1024]{2,1,0:T(8,128)S(1)} %copy-done.1, ...), kind=kLoop, calls=%fused_computation.4 | loop fusion | flops 14680064 | bytes 17432576 | tf_op jit(solution)/shard_map/mul | solution.py:48
  77.4 0.0 copy-start.3
  77.4 2.3 %collective-permute-start.6 = (f32[1,64,1024]{2,1,0:T(8,128)S(1)}, f32[1,64,1024]{2,1,0:T(8,128)S(1)}, u32[]{:S(2)}, u32[]{:S(2)}) collective-permute-start(f32[1,64,1024]{2,1,0:T(8,128)S(1)} %get-tuple-element.15), channel_id=1, source_target_pairs={{0,8},{8,16},{16,24},{24,32},{32,40},{40,48},{48,56},{56,64},{64,7... | collective-permute-start | bytes 786440 | tf_op jit(solution)/shard_map/ppermute | solution.py:22
  79.7 0.0 collective-permute-start.7
  79.7 0.1 multiply_multiply_fusion.1
  79.8 0.1 fusion.28
  79.9 0.0 copy-start.9
  79.9 5.3 %collective-permute-done.6 = f32[1,64,1024]{2,1,0:T(8,128)S(1)} collective-permute-done((f32[1,64,1024]{2,1,0:T(8,128)S(1)}, f32[1,64,1024]{2,1,0:T(8,128)S(1)}, u32[]{:S(2)}, u32[]{:S(2)}) %collective-permute-start.6) | collective-permute-done | bytes 262176 | tf_op jit(solution)/shard_map/ppermute | solution.py:22
  85.2 1.8 %collective-permute-done.7 = f32[1,64,1024]{2,1,0:T(8,128)S(1)} collective-permute-done((f32[1,64,1024]{2,1,0:T(8,128)S(1)}, f32[1,64,1024]{2,1,0:T(8,128)S(1)}, u32[]{:S(2)}, u32[]{:S(2)}) %collective-permute-start.7) | collective-permute-done | bytes 262176 | tf_op jit(solution)/shard_map/ppermute | solution.py:23
  87.0 0.9 fusion.11
  87.9 0.0 copy-done.3
  87.9 0.0 copy-start.6
  87.9 0.1 fusion.45
  88.0 1.8 %copy-done.6 = f32[16,64,1024]{2,1,0:T(8,128)} copy-done((f32[16,64,1024]{2,1,0:T(8,128)}, f32[16,64,1024]{2,1,0:T(8,128)S(1)}, u32[]{:S(2)}) %copy-start.6) | copy-done | bytes 4194328
  89.9 3.3 %collective-permute-start.8 = (f32[16,1,1024]{2,1,0:T(1,128)S(1)}, f32[16,1,1024]{2,1,0:T(1,128)S(1)}, u32[]{:S(2)}, u32[]{:S(2)}) collective-permute-start(f32[16,1,1024]{2,1,0:T(1,128)S(1)} %get-tuple-element.13), channel_id=1, source_target_pairs={{0,1},{1,2},{2,3},{3,4},{4,5},{5,6},{6,7},{8,9},{9,10},{10,11},{11... | collective-permute-start | bytes 196616 | tf_op jit(solution)/shard_map/ppermute | solution.py:22
  93.2 1.5 %collective-permute-start.9 = (f32[16,1,1024]{2,1,0:T(1,128)S(1)}, f32[16,1,1024]{2,1,0:T(1,128)S(1)}, u32[]{:S(2)}, u32[]{:S(2)}) collective-permute-start(f32[16,1,1024]{2,1,0:T(1,128)S(1)} %get-tuple-element.14), channel_id=1, source_target_pairs={{1,0},{2,1},{3,2},{4,3},{5,4},{6,5},{7,6},{9,8},{10,9},{11,10},{12... | collective-permute-start | bytes 196616 | tf_op jit(solution)/shard_map/ppermute | solution.py:23
  94.7 0.0 copy-done.9
  94.7 0.3 collective-permute-done.8
  95.0 3.2 %collective-permute-done.9 = f32[16,1,1024]{2,1,0:T(1,128)S(1)} collective-permute-done((f32[16,1,1024]{2,1,0:T(1,128)S(1)}, f32[16,1,1024]{2,1,0:T(1,128)S(1)}, u32[]{:S(2)}, u32[]{:S(2)}) %collective-permute-start.9) | collective-permute-done | bytes 65568 | tf_op jit(solution)/shard_map/ppermute | solution.py:23
  98.2 1.3 %broadcast_select_fusion.1 = (f32[16,1,1024]{2,1,0:T(1,128)S(1)}, f32[16,1,1024]{2,1,0:T(1,128)S(1)}) fusion(f32[16,1,1024]{2,1,0:T(1,128)S(1)} %collective-permute-done.8, pred[]{:T(512)S(6)} %eq.6, f32[16,64,1024]{2,1,0:T(8,128)} %copy-done.6, f32[16,1,1024]{2,1,0:T(1,128)S(1)} %collective-permute-done.9, pred[]{:T(512)S(6)} %eq.7), kind=kLoop, calls=%fused_computation.57 | loop fusion | flops 32768 | bytes 393218 | tf_op jit(solution)/shard_map/jit(_where)/select_n | solution.py:58
  99.6 0.0 copy-start.4
  99.6 6.5 %fusion.9 = f32[16,64,1024]{2,1,0:T(8,128)S(1)} fusion(f32[16,1,1024]{2,1,0:T(1,128)S(1)} %get-tuple-element.12, f32[16,64,1024]{2,1,0:T(8,128)} %copy-done.6, f32[16,1,1024]{2,1,0:T(1,128)S(1)} %get-tuple-element.11), kind=kLoop, calls=%fused_computation.14 | loop fusion | flops 4194304 | bytes 8519680 | tf_op jit(solution)/shard_map/max | solution.py:61
  106.1 0.2 fusion.44
  106.3 0.0 copy-done.4
  106.3 3.4 %fusion.7 = f32[16,64,1024]{2,1,0:T(8,128)S(1)} fusion(f32[16,64,1024]{2,1,0:T(8,128)S(1)} %copy-done.4, f32[16,64,1]{2,1,0:T(8,128)S(1)} %get-tuple-element.10, f32[16,64,1024]{2,1,0:T(8,128)S(1)} %fusion.9, f32[16,64,1]{2,1,0:T(8,128)S(1)} %get-tuple-element.9, f32[64]{0:T(128)S(1)} %convert_multiply_fusion), kind=kLoop, calls=%fused_computation.10 | loop fusion | flops 9437184 | bytes 12591360 | tf_op jit(solution)/shard_map/mul | solution.py:88
  109.7 0.0 copy-start.7
  109.7 6.2 %fusion.21 = f32[64,16,64]{2,0,1:T(8,128)S(1)} fusion(f32[16,64,1024]{2,1,0:T(8,128)S(1)} %fusion.7, f32[32,1024]{1,0:T(8,128)S(1)} %get-tuple-element.31, f32[32,1024]{1,0:T(8,128)S(1)} %get-tuple-element.30), kind=kOutput, calls=%fused_computation.44 | convolution fusion | flops 805371904 | bytes 4718592 | tf_op jit(solution)/shard_map/frc,kc->kfr/dot_general | solution.py:97
  115.9 0.3 multiply_reduce_fusion.1
  116.2 0.6 maximum_multiply_fusion
  116.8 0.0 copy-done.7
  (6 shorter events, 0.1 us)
Async XLA Ops:
  0.6 30.0 %copy-start.5 = (f32[16,64,1024]{2,1,0:T(8,128)S(1)}, f32[16,64,1024]{2,1,0:T(8,128)}, u32[]{:S(2)}) copy-start(f32[16,64,1024]{2,1,0:T(8,128)} %param.3) | copy-start | bytes 12582916
  2.5 28.0 %collective-permute-start = (f32[4,64,1024]{2,1,0:T(8,128)S(1)}, f32[4,64,1024]{2,1,0:T(8,128)S(1)}, u32[]{:S(2)}, u32[]{:S(2)}) collective-permute-start(f32[4,64,1024]{2,1,0:T(8,128)S(1)} %get-tuple-element.23), channel_id=1, source_target_pairs={{0,8},{8,16},{16,24},{24,32},{32,40},{40,48},{48,56},{56,64},{64,7... | collective-permute-start | bytes 3145736 | tf_op jit(solution)/shard_map/ppermute | solution.py:22
  7.5 25.1 %collective-permute-start.1 = (f32[4,64,1024]{2,1,0:T(8,128)S(1)}, f32[4,64,1024]{2,1,0:T(8,128)S(1)}, u32[]{:S(2)}, u32[]{:S(2)}) collective-permute-start(f32[4,64,1024]{2,1,0:T(8,128)S(1)} %get-tuple-element.24), channel_id=1, source_target_pairs={{8,0},{16,8},{24,16},{32,24},{40,32},{48,40},{56,48},{64,56},{72,6... | collective-permute-start | bytes 3145736 | tf_op jit(solution)/shard_map/ppermute | solution.py:23
  31.5 2.3 %copy-start.2 = (f32[20,64,1024]{2,1,0:T(8,128)}, f32[20,64,1024]{2,1,0:T(8,128)S(1)}, u32[]{:S(2)}) copy-start(f32[20,64,1024]{2,1,0:T(8,128)S(1)} %get-tuple-element.21) | copy-start | bytes 15728644
  33.8 14.8 %copy-start.8 = (s32[3,32]{1,0:T(4,128)S(1)}, s32[3,32]{1,0:T(4,128)}, u32[]{:S(2)}) copy-start(s32[3,32]{1,0:T(4,128)} %param.5) | copy-start | bytes 1156
  42.5 2.0 %copy-start = (f32[16,64,1024]{2,1,0:T(8,128)}, f32[16,64,1024]{2,1,0:T(8,128)S(1)}, u32[]{:S(2)}) copy-start(f32[16,64,1024]{2,1,0:T(8,128)S(1)} %fusion.18) | copy-start | bytes 12582916
  44.5 7.8 %collective-permute-start.2 = (f32[1,64,1024]{2,1,0:T(8,128)S(1)}, f32[1,64,1024]{2,1,0:T(8,128)S(1)}, u32[]{:S(2)}, u32[]{:S(2)}) collective-permute-start(f32[1,64,1024]{2,1,0:T(8,128)S(1)} %get-tuple-element.19), channel_id=1, source_target_pairs={{0,8},{8,16},{16,24},{24,32},{32,40},{40,48},{48,56},{56,64},{64,7... | collective-permute-start | bytes 786440 | tf_op jit(solution)/shard_map/ppermute | solution.py:22
  48.6 7.3 %collective-permute-start.3 = (f32[1,64,1024]{2,1,0:T(8,128)S(1)}, f32[1,64,1024]{2,1,0:T(8,128)S(1)}, u32[]{:S(2)}, u32[]{:S(2)}) collective-permute-start(f32[1,64,1024]{2,1,0:T(8,128)S(1)} %get-tuple-element.20), channel_id=1, source_target_pairs={{8,0},{16,8},{24,16},{32,24},{40,32},{48,40},{56,48},{64,56},{72,6... | collective-permute-start | bytes 786440 | tf_op jit(solution)/shard_map/ppermute | solution.py:23
  48.6 21.0 %copy-start.1 = (f32[16,64,1024]{2,1,0:T(8,128)S(1)}, f32[16,64,1024]{2,1,0:T(8,128)}, u32[]{:S(2)}) copy-start(f32[16,64,1024]{2,1,0:T(8,128)} %copy-done) | copy-start | bytes 12582916
  61.6 4.1 %collective-permute-start.4 = (f32[16,1,1024]{2,1,0:T(1,128)S(1)}, f32[16,1,1024]{2,1,0:T(1,128)S(1)}, u32[]{:S(2)}, u32[]{:S(2)}) collective-permute-start(f32[16,1,1024]{2,1,0:T(1,128)S(1)} %get-tuple-element.17), channel_id=1, source_target_pairs={{0,1},{1,2},{2,3},{3,4},{4,5},{5,6},{6,7},{8,9},{9,10},{10,11},{11... | collective-permute-start | bytes 196616 | tf_op jit(solution)/shard_map/ppermute | solution.py:22
  64.3 5.3 %collective-permute-start.5 = (f32[16,1,1024]{2,1,0:T(1,128)S(1)}, f32[16,1,1024]{2,1,0:T(1,128)S(1)}, u32[]{:S(2)}, u32[]{:S(2)}) collective-permute-start(f32[16,1,1024]{2,1,0:T(1,128)S(1)} %get-tuple-element.18), channel_id=1, source_target_pairs={{1,0},{2,1},{3,2},{4,3},{5,4},{6,5},{7,6},{9,8},{10,9},{11,10},{12... | collective-permute-start | bytes 196616 | tf_op jit(solution)/shard_map/ppermute | solution.py:23
  77.4 10.6 %copy-start.3 = (f32[16,64,1024]{2,1,0:T(8,128)}, f32[16,64,1024]{2,1,0:T(8,128)S(1)}, u32[]{:S(2)}) copy-start(f32[16,64,1024]{2,1,0:T(8,128)S(1)} %fusion.2) | copy-start | bytes 12582916
  77.4 7.8 %collective-permute-start.6 = (f32[1,64,1024]{2,1,0:T(8,128)S(1)}, f32[1,64,1024]{2,1,0:T(8,128)S(1)}, u32[]{:S(2)}, u32[]{:S(2)}) collective-permute-start(f32[1,64,1024]{2,1,0:T(8,128)S(1)} %get-tuple-element.15), channel_id=1, source_target_pairs={{0,8},{8,16},{16,24},{24,32},{32,40},{40,48},{48,56},{56,64},{64,7... | collective-permute-start | bytes 786440 | tf_op jit(solution)/shard_map/ppermute | solution.py:22
  79.7 7.3 %collective-permute-start.7 = (f32[1,64,1024]{2,1,0:T(8,128)S(1)}, f32[1,64,1024]{2,1,0:T(8,128)S(1)}, u32[]{:S(2)}, u32[]{:S(2)}) collective-permute-start(f32[1,64,1024]{2,1,0:T(8,128)S(1)} %get-tuple-element.16), channel_id=1, source_target_pairs={{8,0},{16,8},{24,16},{32,24},{40,32},{48,40},{56,48},{64,56},{72,6... | collective-permute-start | bytes 786440 | tf_op jit(solution)/shard_map/ppermute | solution.py:23
  79.9 14.8 %copy-start.9 = (s32[64]{0:T(128)S(1)}, s32[64]{0:T(128)}, u32[]{:S(2)}) copy-start(s32[64]{0:T(128)} %param.4) | copy-start | bytes 772
  87.9 2.0 %copy-start.6 = (f32[16,64,1024]{2,1,0:T(8,128)}, f32[16,64,1024]{2,1,0:T(8,128)S(1)}, u32[]{:S(2)}) copy-start(f32[16,64,1024]{2,1,0:T(8,128)S(1)} %fusion.11) | copy-start | bytes 12582916
  89.9 5.2 %collective-permute-start.8 = (f32[16,1,1024]{2,1,0:T(1,128)S(1)}, f32[16,1,1024]{2,1,0:T(1,128)S(1)}, u32[]{:S(2)}, u32[]{:S(2)}) collective-permute-start(f32[16,1,1024]{2,1,0:T(1,128)S(1)} %get-tuple-element.13), channel_id=1, source_target_pairs={{0,1},{1,2},{2,3},{3,4},{4,5},{5,6},{6,7},{8,9},{9,10},{10,11},{11... | collective-permute-start | bytes 196616 | tf_op jit(solution)/shard_map/ppermute | solution.py:22
  93.2 5.0 %collective-permute-start.9 = (f32[16,1,1024]{2,1,0:T(1,128)S(1)}, f32[16,1,1024]{2,1,0:T(1,128)S(1)}, u32[]{:S(2)}, u32[]{:S(2)}) collective-permute-start(f32[16,1,1024]{2,1,0:T(1,128)S(1)} %get-tuple-element.14), channel_id=1, source_target_pairs={{1,0},{2,1},{3,2},{4,3},{5,4},{6,5},{7,6},{9,8},{10,9},{11,10},{12... | collective-permute-start | bytes 196616 | tf_op jit(solution)/shard_map/ppermute | solution.py:23
  99.6 6.7 %copy-start.4 = (f32[16,64,1024]{2,1,0:T(8,128)S(1)}, f32[16,64,1024]{2,1,0:T(8,128)}, u32[]{:S(2)}) copy-start(f32[16,64,1024]{2,1,0:T(8,128)} %copy-done.3) | copy-start | bytes 12582916
  109.7 7.1 %copy-start.7 = (f32[16,64,1024]{2,1,0:T(8,128)}, f32[16,64,1024]{2,1,0:T(8,128)S(1)}, u32[]{:S(2)}) copy-start(f32[16,64,1024]{2,1,0:T(8,128)S(1)} %fusion.7) | copy-start | bytes 12582916
where the time goes:
time: 117 us
  waiting for transfers between devices  45.9 us (39%)
  other arithmetic  35.3 us (30%)
  starting transfers between devices  20.1 us (17%)
  local copies, waits for them, and re-layouts  8.35 us (7%)
  matrix products  6.18 us (5%)
    ppermute x5, waiting for transfers between devices, extended_2(): before = lax.ppermute(last, axis, up)  32.5 us
    ppermute x5, starting transfers between devices, extended_2(): before = lax.ppermute(last, axis, up)  17.3 us
    ppermute x5, waiting for transfers between devices, extended_2(): after = lax.ppermute(leading, axis, down)  13.4 us
    sub x1, other arithmetic, on_device(): corrected = frames - total / span  8.68 us
    max x1, other arithmetic, row_maxima(): return jnp.maximum(jnp.maximum(fixed[:, :-2], fixed[:, 1:-1]), fixed[:, 2:])  6.46 us
    dot_general x1, matrix products, on_device(): jnp.einsum('frc,kc->kfr', weight, stacked, precision=lax.Precision.HIGHEST)  6.18 us
    mul x1, other arithmetic, frame_filter(): return (padded[:-2] + 2.0 * padded[1:-1] + padded[2:]) * 0.25  5.63 us
    unnamed x21, local copies, waits for them, and re-layouts  5.12 us
  transfers between devices with their start and end apart: 10, of which 10 were waited for; matrix products, arithmetic and copies ran while one was open for 1% of the time, Pallas kernels for 0%

commit v1 on v0

v1 whole, which is shorter than its diff:
```python
import functools

import jax
import jax.numpy as jnp
from jax import lax
from jax.experimental import pallas as pl
from jax.experimental.pallas import tpu as pltpu
from jax.sharding import PartitionSpec as P

BW = 4
REACH = BW + 2
BOX_F = 8
BOX_R = 16
BOX_C = 16
SHARP = 8.0
LOG2E = 1.4426950408889634
BIG = 3.0e38
LANES = 128
DEPTH = 3
LATE = 4
MESH = pl.DeviceIdType.MESH


def spread_kernel(n_omega, n_row, frames, thresholds, weight, x, first, second, smooth, wide, level, outgoing, incoming, load_sem, send_sem, recv_sem, row_send, row_recv):
    depth, rows = (frames.shape[0], frames.shape[1])
    tiles = frames.shape[2] // LANES
    groups = rows // 8
    planes = depth + 2
    omega, row = (lax.axis_index("omega"), lax.axis_index("row"))
    after, before = (lax.rem(omega + 1, n_omega), lax.rem(omega + n_omega - 1, n_omega))
    has_upper, has_lower = (row > 0, row < n_row - 1)

    def load(t):
        return pltpu.make_async_copy(frames.at[:, :, pl.ds(t * LANES, LANES)], x.at[pl.ds(REACH, depth), t], load_sem.at[t])

    for t in range(tiles):
        load(t).start()

    barrier = pltpu.get_barrier_semaphore()
    for neighbour in (before, after):
        pl.semaphore_signal(barrier, inc=1, device_id=(neighbour, row), device_id_type=MESH)

    @pl.when(has_upper)
    def _():
        pl.semaphore_signal(barrier, inc=1, device_id=(omega, row - 1), device_id_type=MESH)

    @pl.when(has_lower)
    def _():
        pl.semaphore_signal(barrier, inc=1, device_id=(omega, row + 1), device_id_type=MESH)

    sub = lax.broadcasted_iota(jnp.int32, (8, LANES), 0)
    lane = lax.broadcasted_iota(jnp.int32, (8, LANES), 1)
    for g in range(groups):
        tile = jnp.full((8, LANES), thresholds[g * 8].astype(jnp.float32))
        for j in range(1, 8):
            tile = jnp.where(sub == j, thresholds[g * 8 + j].astype(jnp.float32), tile)
        level[g * 8 : g * 8 + 8, :] = tile
    blank = jnp.zeros((rows + 8, LANES), jnp.float32)
    for i in range(planes):
        second[i, 0] = blank
        second[i, tiles + 1] = blank

    def piece(start, chunk):
        planes_of = pl.ds(start, REACH)
        if isinstance(chunk, int) and chunk < 2:
            return x.at[planes_of, :, pl.ds(0 if chunk == 0 else rows - 8, 8), :]
        return x.at[planes_of, chunk - 2, pl.ds(8, rows - 16), :]

    def copies(chunk):
        to_before = pltpu.make_async_remote_copy(
            src_ref=piece(REACH, chunk), dst_ref=piece(REACH + depth, chunk), send_sem=send_sem.at[0, chunk], recv_sem=recv_sem.at[0, chunk], device_id=(before, row), device_id_type=MESH
        )
        to_after = pltpu.make_async_remote_copy(
            src_ref=piece(depth, chunk), dst_ref=piece(0, chunk), send_sem=send_sem.at[1, chunk], recv_sem=recv_sem.at[1, chunk], device_id=(after, row), device_id_type=MESH
        )
        return (to_before, to_after)

    def row_copy(side):
        return pltpu.make_async_remote_copy(
            src_ref=outgoing.at[side], dst_ref=incoming.at[side], send_sem=row_send.at[side], recv_sem=row_recv.at[side], device_id=(omega, row - 1 if side == 0 else row + 1), device_id_type=MESH
        )

    for t in range(tiles):
        load(t).wait()
    pl.semaphore_wait(barrier, 2 + has_upper.astype(jnp.int32) + has_lower.astype(jnp.int32))

    def issue(chunk):
        for copy in copies(chunk):
            copy.start()

    def arrive(chunk):
        for copy in copies(chunk):
            copy.wait_recv()
        for copy in copies(chunk):
            copy.wait_send()

    def frame_stage(t, start):
        v = [x[j, t, pl.ds(start, 8), :] for j in range(depth + 2 * REACH)]
        s2 = [v[j] + v[j + 1] for j in range(len(v) - 1)]
        s4 = [s2[j] + s2[j + 2] for j in range(len(s2) - 2)]
        s8 = [s4[j] + s4[j + 4] for j in range(len(s4) - 4)]
        c = [v[j + BW] - (s8[j] + v[j + 2 * BW]) * (1.0 / (2 * BW + 1)) for j in range(depth + 4)]
        p = [c[j] + c[j + 1] for j in range(depth + 3)]
        for i in range(planes):
            first[i, t, pl.ds(start + 8, 8), :] = p[i] + p[i + 1]

    def row_stage(t):
        def body(k, carry):
            for i in range(planes):
                up = first[i, t, pl.ds(8 * k + 6, 8), :]
                mid = first[i, t, pl.ds(8 * k + 7, 8), :]
                down = first[i, t, pl.ds(8 * k + 8, 8), :]
                second[i, t + 1, pl.ds(pl.multiple_of(8 * k, 8), 8), :] = (up + down) + (mid + mid)
            return carry

        lax.fori_loop(0, groups + 1, body, 0)

    def column_stage(t):
        left_edge, right_edge = (lane == 0, lane == LANES - 1)
        left_half = lane >= LANES // 2
        low = jnp.where(t == 0, -BIG, BIG)
        high = jnp.where(t == tiles - 1, -BIG, BIG)
        bound = jnp.where(left_half, low, high)

        def body(k, carry):
            at = pl.ds(pl.multiple_of(8 * k, 8), 8)
            for i in range(planes):
                a, b, c = (second[i, t, at, :], second[i, t + 1, at, :], second[i, t + 2, at, :])
                w = jnp.where(left_half, a, c)
                to_right = pltpu.roll(jnp.where(right_edge, a, b), 1, 1)
                to_left = pltpu.roll(jnp.where(left_edge, c, b), LANES - 1, 1)
                value = (to_right + to_left) + (b + b)
                w_right = pltpu.roll(jnp.where(right_edge, b, w), 1, 1)
                w_left = pltpu.roll(jnp.where(left_edge, b, w), LANES - 1, 1)
                beside = jnp.minimum((w_right + w_left) + (w + w), bound)
                from_left = pltpu.roll(jnp.where(right_edge, beside, value), 1, 1)
                from_right = pltpu.roll(jnp.where(left_edge, beside, value), LANES - 1, 1)
                wide[i, at, :] = jnp.maximum(jnp.maximum(from_left, from_right), value)
                if 0 < i < planes - 1:
                    smooth[i - 1, at, :] = value
            return carry

        lax.fori_loop(0, groups + 1, body, 0)

        @pl.when(jnp.logical_not(has_upper))
        def _():
            for i in range(planes):
                wide[i, 0:1, :] = jnp.full((1, LANES), -BIG)

        @pl.when(jnp.logical_not(has_lower))
        def _():
            for i in range(planes):
                wide[i, rows + 1 : rows + 2, :] = jnp.full((1, LANES), -BIG)

    def weight_stage(t):
        def body(g, carry):
            start = pl.multiple_of(8 * g, 8)
            limit = level[pl.ds(start, 8), :]
            tall = []
            for i in range(planes):
                up = wide[i, pl.ds(8 * g, 8), :]
                mid = wide[i, pl.ds(8 * g + 1, 8), :]
                down = wide[i, pl.ds(8 * g + 2, 8), :]
                tall.append(jnp.maximum(jnp.maximum(up, down), mid))
                if i >= 2:
                    highest = jnp.maximum(jnp.maximum(tall[i - 2], tall[i - 1]), tall[i])
                    value = smooth[i - 2, pl.ds(8 * g + 1, 8), :]
                    sharp = jnp.exp2((value - highest) * (SHARP * LOG2E / 64.0))
                    weight[i - 2, t, pl.ds(start, 8), :] = sharp * (jnp.maximum(value - limit, 0.0) * (1.0 / 64.0))
            return carry

        lax.fori_loop(0, groups, body, 0)

    def finish(t):
        column_stage(t)
        weight_stage(t)

    for chunk in range(DEPTH):
        issue(chunk)

    def edge(side):
        arrive(side)
        issue(side + DEPTH)
        start = 0 if side == 0 else rows - 8

        def body(t, carry):
            frame_stage(t, start)
            for i in range(planes):
                outgoing[side, pl.ds((i * tiles + t) * 2, 2), :] = first[i, t, pl.ds(8 if side == 0 else rows + 6, 2), :]
            return carry

        lax.fori_loop(0, tiles, body, 0)

        @pl.when(has_upper if side == 0 else has_lower)
        def _():
            row_copy(side).start()

    edge(0)
    edge(1)

    def take(t):
        arrive(t + 2)

        @pl.when(t + 2 + DEPTH < tiles + 2)
        def _():
            issue(t + 2 + DEPTH)

        def body(g, carry):
            frame_stage(t, pl.multiple_of(8 * g, 8))
            return carry

        lax.fori_loop(1, groups - 1, body, 0)

    def early(t, carry):
        take(t)
        return carry

    lax.fori_loop(0, LATE + 1, early, 0)

    for side in range(2):
        place = rows + 8 if side == 0 else 6
        there = has_lower if side == 0 else has_upper

        @pl.when(there)
        def _():
            row_copy(side).wait_recv()

            def body(t, carry):
                for i in range(planes):
                    first[i, t, pl.ds(place, 2), :] = incoming[side, pl.ds((i * tiles + t) * 2, 2), :]
                return carry

            lax.fori_loop(0, tiles, body, 0)

        @pl.when(jnp.logical_not(there))
        def _():
            def body(t, carry):
                for i in range(planes):
                    first[i, t, pl.ds(place, 2), :] = jnp.zeros((2, LANES), jnp.float32)
                return carry

            lax.fori_loop(0, tiles, body, 0)

    row_stage(0)

    def catch_up(t, carry):
        row_stage(t + 1)
        finish(t)
        return carry

    lax.fori_loop(0, LATE, catch_up, 0)

    def late(t, carry):
        take(t)
        row_stage(t)
        finish(t - 1)
        return carry

    lax.fori_loop(LATE + 1, tiles, late, 0)
    finish(tiles - 1)

    for side in range(2):

        @pl.when(has_upper if side == 0 else has_lower)
        def _():
            row_copy(side).wait_send()


def moments_kernel(boxes, weight, out, moments, parts, sem):
    depth, tiles, rows = weight.shape[0:3]
    slots = boxes.shape[1]

    def store(t):
        return pltpu.make_async_copy(weight.at[:, t], out.at[:, :, pl.ds(t * LANES, LANES)], sem.at[t])

    for t in range(tiles):
        store(t).start()
    frame_base = lax.axis_index("omega") * depth
    row_base = lax.axis_index("row") * rows
    sub = lax.broadcasted_iota(jnp.int32, (8, LANES), 0)
    lane = lax.broadcasted_iota(jnp.int32, (8, LANES), 1)
    half_f, half_r, half_c = ((BOX_F - 1) / 2.0, (BOX_R - 1) / 2.0, (BOX_C - 1) / 2.0)
    u_row = [((sub + 8 * j).astype(jnp.float32) - half_r) / half_r for j in range(2)]

    def box(b, carry):
        live = boxes[0, b] >= 0

        @pl.when(live)
        def _():
            f0 = boxes[0, b] - frame_base
            r0 = boxes[1, b] - row_base
            c0 = boxes[2, b]
            totals = None
            for side in range(2):
                tile = jnp.minimum(c0 // LANES + side, tiles - 1)
                distance = lane - (lax.rem(c0, LANES) - side * LANES)
                inside = (distance >= 0) & (distance < BOX_C)
                u_column = (distance.astype(jnp.float32) - half_c) / half_c
                plain = [None, None]
                framed = [None, None]
                for j in range(2):
                    for i in range(BOX_F):
                        w = weight[f0 + i, tile, pl.ds(r0 + 8 * j, 8), :]
                        m = w * ((i - half_f) / half_f)
                        plain[j] = w if i == 0 else plain[j] + w
                        framed[j] = m if i == 0 else framed[j] + m
                everything = plain[0] + plain[1]
                stats = [everything, framed[0] + framed[1], plain[0] * u_row[0] + plain[1] * u_row[1], everything * u_column]
                stats = [jnp.where(inside, s, 0.0) for s in stats]
                totals = stats if side == 0 else [p + q for p, q in zip(totals, stats)]
            for s in range(4):
                parts[s, pl.ds(pl.multiple_of(b * 8, 8), 8), :] = totals[s]

        @pl.when(jnp.logical_not(live))
        def _():
            for s in range(4):
                parts[s, pl.ds(pl.multiple_of(b * 8, 8), 8), :] = jnp.zeros((8, LANES), jnp.float32)

        return carry

    lax.fori_loop(0, slots, box, 0)
    ones = jnp.ones((8, LANES), jnp.float32)
    lines = []
    for s in range(4):
        total = parts[s, pl.ds(0, slots, stride=8), :]
        for j in range(1, 8):
            total = total + parts[s, pl.ds(j, slots, stride=8), :]
        sums = lax.dot_general(ones, total, (((1,), (1,)), ((), ())), precision=lax.Precision.HIGHEST, preferred_element_type=jnp.float32)
        lines.append(sums[0:1, :])
    moments[...] = jnp.concatenate(lines, axis=0) * (1.0 / (BOX_F * BOX_R * BOX_C))
    for t in range(tiles):
        store(t).wait()


def on_device(n_omega, n_row, frames, thresholds, spot_boxes):
    depth, rows, columns = frames.shape
    tiles = columns // LANES
    planes = depth + 2
    slots = spot_boxes.shape[1]
    vmem = functools.partial(pl.BlockSpec, memory_space=pltpu.VMEM)
    smem = functools.partial(pl.BlockSpec, memory_space=pltpu.SMEM)
    anywhere = functools.partial(pl.BlockSpec, memory_space=pl.ANY)
    weight = pl.pallas_call(
        functools.partial(spread_kernel, n_omega, n_row),
        out_shape=pltpu.VMEM((depth, tiles, rows, LANES), jnp.float32),
        in_specs=[pl.BlockSpec(memory_space=pltpu.HBM), smem()],
        out_specs=vmem(),
        scratch_shapes=[
            pltpu.VMEM((depth + 2 * REACH, tiles, rows, LANES), jnp.float32),
            pltpu.VMEM((planes, tiles, rows + 16, LANES), jnp.float32),
            pltpu.VMEM((planes, tiles + 2, rows + 8, LANES), jnp.float32),
            pltpu.VMEM((depth, rows + 8, LANES), jnp.float32),
            pltpu.VMEM((planes, rows + 8, LANES), jnp.float32),
            pltpu.VMEM((rows, LANES), jnp.float32),
            pltpu.VMEM((2, planes * tiles * 2, LANES), jnp.float32),
            pltpu.VMEM((2, planes * tiles * 2, LANES), jnp.float32),
            pltpu.SemaphoreType.DMA((tiles,)),
            pltpu.SemaphoreType.DMA((2, tiles + 2)),
            pltpu.SemaphoreType.DMA((2, tiles + 2)),
            pltpu.SemaphoreType.DMA((2,)),
            pltpu.SemaphoreType.DMA((2,)),
        ],
        compiler_params=pltpu.CompilerParams(collective_id=0, has_side_effects=True, vmem_limit_bytes=32 << 20),
        name="spread",
    )(frames, thresholds)
    return pl.pallas_call(
        moments_kernel,
        out_shape=(jax.ShapeDtypeStruct(frames.shape, jnp.float32), jax.ShapeDtypeStruct((4, slots), jnp.float32)),
        in_specs=[smem(), vmem()],
        out_specs=(anywhere(), vmem()),
        scratch_shapes=[pltpu.VMEM((4, slots * 8, LANES), jnp.float32), pltpu.SemaphoreType.DMA((tiles,))],
        compiler_params=pltpu.CompilerParams(vmem_limit_bytes=8 << 20),
        name="moments",
    )(spot_boxes, weight)


def solution(mesh):
    return jax.shard_map(
        functools.partial(on_device, mesh.shape["omega"], mesh.shape["row"]),
        mesh=mesh,
        in_specs=(P("omega", "row", None), P("row"), P(None, ("omega", "row"))),
        out_specs=(P("omega", "row", None), P(None, ("omega", "row"))),
        check_vma=False,
    )
```

time: 117 us -> 75.5 us (0.65)
  Pallas kernels: 0 us -> 71.8 us
  waiting for transfers between devices: 45.9 us -> 0 us
  other arithmetic: 35.3 us -> 0 us
  starting transfers between devices: 20.1 us -> 0 us
  matrix products: 6.18 us -> 0 us
  local copies, waits for them, and re-layouts: 8.35 us -> 2.84 us
    pallas_call x0 -> x2, Pallas kernels: none -> 71.8 us  [the longest x1 68.6 us: on_device(): pl.pallas_call(functools.partial(spread_kernel, n_omega, n_row), out_shap...]
    ppermute x10 -> x0, waiting for transfers between devices: 45.9 us -> none  [the longest x5 32.5 us: extended_2(): before = lax.ppermute(last, axis, up)]
    ppermute x10 -> x0, starting transfers between devices: 20.1 us -> none  [the longest x5 17.3 us: extended_2(): before = lax.ppermute(last, axis, up)]
    mul x5 -> x0, other arithmetic: 16.9 us -> none  [the longest x1 5.63 us: frame_filter(): return (padded[:-2] + 2.0 * padded[1:-1] + padded[2:]) * 0.25]
    sub x2 -> x0, other arithmetic: 8.68 us -> none  [the longest x1 8.68 us: on_device(): corrected = frames - total / span]
    max x2 -> x0, other arithmetic: 7.38 us -> none  [the longest x1 6.46 us: row_maxima(): return jnp.maximum(jnp.maximum(fixed[:, :-2], fixed[:, 1:-1]), fixed[:, 2:])]
    dot_general x1 -> x0, matrix products: 6.18 us -> none  [on_device(): jnp.einsum('frc,kc->kfr', weight, stacked, precision=lax.Precision.HIGHEST)]
    slice x6 -> x0, local copies, waits for them, and re-layouts: 2.31 us -> none  [the longest x5 2.1 us: extended_2(): last = lax.slice_in_dim(x, length - width, length, axis=dim)]
  transfers between devices with their start and end apart: 10 -> 0, of which waited for: 10 -> 0; matrix products, arithmetic and copies ran while one was open for 1% -> 0% of each run, Pallas kernels for 0% -> 0%
where the time goes in v1:
time: 75.5 us; the launch traced here: 75.3 us
  Pallas kernels  71.8 us (95%)
  local copies, waits for them, and re-layouts  2.84 us (4%)
    pallas_call x1, Pallas kernels, on_device(): pl.pallas_call(functools.partial(spread_kernel, n_omega, n_row), out_shap...  68.6 us
    pallas_call x1, Pallas kernels, on_device(): pl.pallas_call(moments_kernel, out_shape=(jax.ShapeDtypeStruct(frames.sha...  3.21 us
    unnamed x6, local copies, waits for them, and re-layouts  2.84 us

profile of v1, /device:TPU:1, one launch (start us, length us, event | category | flops | bytes accessed | tf_op | source)
XLA Modules:
  0.0 75.3 jit_solution(7817982927920290534)
XLA Ops:
  0.6 0.0 copy-start
  0.6 2.2 %copy-done = f32[16,64,1024]{2,1,0:T(8,128)S(1)} copy-done((f32[16,64,1024]{2,1,0:T(8,128)S(1)}, f32[16,64,1024]{2,1,0:T(8,128)}, u32[]{:S(2)}) %copy-start) | copy-done | bytes 4194328
  2.8 0.0 copy-start.2
  2.8 0.7 copy-done.2
  3.5 0.0 copy-start.1
  3.5 68.6 %spread.1.weight = f32[16,8,64,128]{3,2,1,0:T(8,128)S(1)} custom-call(f32[16,64,1024]{2,1,0:T(8,128)S(1)} %copy-done, s32[64]{0:T(128)S(1)} %copy-done.2), custom_call_target="tpu_custom_call" | custom-call | tf_op jit(solution)/shard_map/spread/pallas_call | solution.py:343
  72.1 0.0 copy-done.1
  72.1 3.2 %moments.1 = (f32[16,64,1024]{2,1,0:T(8,128)}, f32[4,32]{1,0:T(4,128)}) custom-call(s32[3,32]{1,0:T(4,128)S(1)} %copy-done.1, f32[16,8,64,128]{3,2,1,0:T(8,128)S(1)} %spread.1.weight), custom_call_target="tpu_custom_call" | custom-call | tf_op jit(solution)/shard_map/moments/pallas_call | solution.py:366
Async XLA Ops:
  0.6 2.2 %copy-start = (f32[16,64,1024]{2,1,0:T(8,128)S(1)}, f32[16,64,1024]{2,1,0:T(8,128)}, u32[]{:S(2)}) copy-start(f32[16,64,1024]{2,1,0:T(8,128)} %frames.1) | copy-start | bytes 12582916
  2.8 0.7 copy-start.2
  3.5 68.6 %copy-start.1 = (s32[3,32]{1,0:T(4,128)S(1)}, s32[3,32]{1,0:T(4,128)}, u32[]{:S(2)}) copy-start(s32[3,32]{1,0:T(4,128)} %boxes.1) | copy-start | bytes 1156

commit v2 on v1

--- a/solution.py
+++ b/solution.py
@@ -21,7 +21,7 @@
 MESH = pl.DeviceIdType.MESH
 
 
-def spread_kernel(n_omega, n_row, frames, thresholds, weight, x, first, second, smooth, wide, level, outgoing, incoming, load_sem, send_sem, recv_sem, row_send, row_recv):
+def spread_kernel(n_omega, n_row, frames, limits, weight, thresholds, x, first, second, smooth, wide, level, outgoing, incoming, limit_sem, load_sem, send_sem, recv_sem, row_send, row_recv):
     depth, rows = (frames.shape[0], frames.shape[1])
     tiles = frames.shape[2] // LANES
     groups = rows // 8
@@ -33,6 +33,8 @@
     def load(t):
         return pltpu.make_async_copy(frames.at[:, :, pl.ds(t * LANES, LANES)], x.at[pl.ds(REACH, depth), t], load_sem.at[t])
 
+    limits_copy = pltpu.make_async_copy(limits, thresholds, limit_sem)
+    limits_copy.start()
     for t in range(tiles):
         load(t).start()
 
@@ -50,6 +52,7 @@
 
     sub = lax.broadcasted_iota(jnp.int32, (8, LANES), 0)
     lane = lax.broadcasted_iota(jnp.int32, (8, LANES), 1)
+    limits_copy.wait()
     for g in range(groups):
         tile = jnp.full((8, LANES), thresholds[g * 8].astype(jnp.float32))
         for j in range(1, 8):
@@ -343,9 +346,10 @@
     weight = pl.pallas_call(
         functools.partial(spread_kernel, n_omega, n_row),
         out_shape=pltpu.VMEM((depth, tiles, rows, LANES), jnp.float32),
-        in_specs=[pl.BlockSpec(memory_space=pltpu.HBM), smem()],
+        in_specs=[pl.BlockSpec(memory_space=pltpu.HBM), pl.BlockSpec(memory_space=pltpu.HBM)],
         out_specs=vmem(),
         scratch_shapes=[
+            pltpu.SMEM((rows,), jnp.int32),
             pltpu.VMEM((depth + 2 * REACH, tiles, rows, LANES), jnp.float32),
             pltpu.VMEM((planes, tiles, rows + 16, LANES), jnp.float32),
             pltpu.VMEM((planes, tiles + 2, rows + 8, LANES), jnp.float32),
@@ -354,13 +358,14 @@
             pltpu.VMEM((rows, LANES), jnp.float32),
             pltpu.VMEM((2, planes * tiles * 2, LANES), jnp.float32),
             pltpu.VMEM((2, planes * tiles * 2, LANES), jnp.float32),
+            pltpu.SemaphoreType.DMA,
             pltpu.SemaphoreType.DMA((tiles,)),
             pltpu.SemaphoreType.DMA((2, tiles + 2)),
             pltpu.SemaphoreType.DMA((2, tiles + 2)),
             pltpu.SemaphoreType.DMA((2,)),
             pltpu.SemaphoreType.DMA((2,)),
         ],
-        compiler_params=pltpu.CompilerParams(collective_id=0, has_side_effects=True, vmem_limit_bytes=32 << 20),
+        compiler_params=pltpu.CompilerParams(collective_id=0, has_side_effects=True, vmem_limit_bytes=54 << 20),
         name="spread",
     )(frames, thresholds)
     return pl.pallas_call(

time: 75.5 us -> 72.1 us (0.955)
  local copies, waits for them, and re-layouts: 2.84 us -> 0.01 us
    unnamed x6 -> x2, local copies, waits for them, and re-layouts: 2.84 us -> 0.01 us
where the time goes in v2:
time: 72.1 us; the launch traced here: 72 us
  Pallas kernels  71.4 us (99%)
    pallas_call x1, Pallas kernels, on_device(): pl.pallas_call(functools.partial(spread_kernel, n_omega, n_row), out_shap...  68.2 us
    pallas_call x1, Pallas kernels, on_device(): pl.pallas_call(moments_kernel, out_shape=(jax.ShapeDtypeStruct(frames.sha...  3.21 us

profile of v2, /device:TPU:1, one launch (start us, length us, event | category | flops | bytes accessed | tf_op | source)
XLA Modules:
  0.0 72.0 jit_solution(2636854771049770374)
XLA Ops:
  0.6 0.0 copy-start
  0.6 68.2 %spread.1.weight = f32[16,8,64,128]{3,2,1,0:T(8,128)S(1)} custom-call(f32[16,64,1024]{2,1,0:T(8,128)} %frames.1, s32[64]{0:T(128)} %limits.1), custom_call_target="tpu_custom_call" | custom-call | tf_op jit(solution)/shard_map/spread/pallas_call | solution.py:346
  68.8 0.0 copy-done
  68.8 3.2 %moments.1 = (f32[16,64,1024]{2,1,0:T(8,128)}, f32[4,32]{1,0:T(4,128)}) custom-call(s32[3,32]{1,0:T(4,128)S(1)} %copy-done, f32[16,8,64,128]{3,2,1,0:T(8,128)S(1)} %spread.1.weight), custom_call_target="tpu_custom_call" | custom-call | tf_op jit(solution)/shard_map/moments/pallas_call | solution.py:371
Async XLA Ops:
  0.6 68.2 %copy-start = (s32[3,32]{1,0:T(4,128)S(1)}, s32[3,32]{1,0:T(4,128)}, u32[]{:S(2)}) copy-start(s32[3,32]{1,0:T(4,128)} %boxes.1) | copy-start | bytes 1156

commit v3 on v2

--- a/solution.py
+++ b/solution.py
@@ -17,26 +17,32 @@
 BIG = 3.0e38
 LANES = 128
 DEPTH = 3
-LATE = 4
+LATE = 1
+BLOCK = 6
 MESH = pl.DeviceIdType.MESH
 
 
-def spread_kernel(n_omega, n_row, frames, limits, weight, thresholds, x, first, second, smooth, wide, level, outgoing, incoming, limit_sem, load_sem, send_sem, recv_sem, row_send, row_recv):
+def spread_kernel(n_omega, n_row, frames, limits, weight, thresholds, x, first, second, smooth, wide, level, mix, outgoing, incoming, limit_sem, load_sem, send_sem, recv_sem, row_send, row_recv):
     depth, rows = (frames.shape[0], frames.shape[1])
     tiles = frames.shape[2] // LANES
     groups = rows // 8
     planes = depth + 2
+    tall = rows + 8
     omega, row = (lax.axis_index("omega"), lax.axis_index("row"))
     after, before = (lax.rem(omega + 1, n_omega), lax.rem(omega + n_omega - 1, n_omega))
     has_upper, has_lower = (row > 0, row < n_row - 1)
 
-    def load(t):
-        return pltpu.make_async_copy(frames.at[:, :, pl.ds(t * LANES, LANES)], x.at[pl.ds(REACH, depth), t], load_sem.at[t])
+    def load(part, t):
+        start, count = ((0, 8), (rows - 8, 8), (8, rows - 16))[part]
+        return pltpu.make_async_copy(
+            frames.at[:, pl.ds(start, count), pl.ds(t * LANES, LANES)], x.at[pl.ds(REACH, depth), t, pl.ds(start, count), :], load_sem.at[part, t]
+        )
 
     limits_copy = pltpu.make_async_copy(limits, thresholds, limit_sem)
+    for part in range(3):
+        for t in range(tiles):
+            load(part, t).start()
     limits_copy.start()
-    for t in range(tiles):
-        load(t).start()
 
     barrier = pltpu.get_barrier_semaphore()
     for neighbour in (before, after):
@@ -51,17 +57,35 @@
         pl.semaphore_signal(barrier, inc=1, device_id=(omega, row + 1), device_id_type=MESH)
 
     sub = lax.broadcasted_iota(jnp.int32, (8, LANES), 0)
-    lane = lax.broadcasted_iota(jnp.int32, (8, LANES), 1)
-    limits_copy.wait()
-    for g in range(groups):
-        tile = jnp.full((8, LANES), thresholds[g * 8].astype(jnp.float32))
-        for j in range(1, 8):
-            tile = jnp.where(sub == j, thresholds[g * 8 + j].astype(jnp.float32), tile)
-        level[g * 8 : g * 8 + 8, :] = tile
-    blank = jnp.zeros((rows + 8, LANES), jnp.float32)
-    for i in range(planes):
-        second[i, 0] = blank
-        second[i, tiles + 1] = blank
+
+    def prepare():
+        limits_copy.wait()
+        for g in range(groups):
+            tile = jnp.full((8, LANES), thresholds[g * 8].astype(jnp.float32))
+            for j in range(1, 8):
+                tile = jnp.where(sub == j, thresholds[g * 8 + j].astype(jnp.float32), tile)
+            level[g * 8 : g * 8 + 8, :] = tile
+        blank = jnp.zeros((tall, LANES), jnp.float32)
+        for i in range(planes):
+            second[0, i * tall : (i + 1) * tall, :] = blank
+            second[tiles + 1, i * tall : (i + 1) * tall, :] = blank
+        last = LANES - 1
+        size = (LANES, LANES)
+        source, place = (lax.broadcasted_iota(jnp.int32, size, 0), lax.broadcasted_iota(jnp.int32, size, 1))
+
+        def taps(pairs):
+            total = jnp.zeros(size, jnp.float32)
+            for test, value in pairs:
+                total = total + jnp.where(test, value, 0.0)
+            return total.astype(jnp.bfloat16)
+
+        at_first, at_last = (place == 0, place == last)
+        mix[0:LANES, 0:LANES] = taps([(source == place, 2.0), (source == place - 1, 1.0), (source == place + 1, 1.0)])
+        mix[LANES:, 0:LANES] = taps([(at_first & (source == last), 1.0), (at_last & (source == 0), 1.0)])
+        mix[0:LANES, LANES:] = taps([(at_first & (source == last), 1.0), (at_last & (source == 0), 1.0)])
+        mix[LANES:, LANES:] = taps(
+            [(at_first & (source == 0), 2.0), (at_first & (source == 1), 1.0), (at_last & (source == last), 2.0), (at_last & (source == last - 1), 1.0)]
+        )
 
     def piece(start, chunk):
         planes_of = pl.ds(start, REACH)
@@ -84,7 +108,7 @@
         )
 
     for t in range(tiles):
-        load(t).wait()
+        load(0, t).wait()
     pl.semaphore_wait(barrier, 2 + has_upper.astype(jnp.int32) + has_lower.astype(jnp.int32))
 
     def issue(chunk):
@@ -113,61 +137,60 @@
                 up = first[i, t, pl.ds(8 * k + 6, 8), :]
                 mid = first[i, t, pl.ds(8 * k + 7, 8), :]
                 down = first[i, t, pl.ds(8 * k + 8, 8), :]
-                second[i, t + 1, pl.ds(pl.multiple_of(8 * k, 8), 8), :] = (up + down) + (mid + mid)
+                second[t + 1, pl.ds(pl.multiple_of(i * tall + 8 * k, 8), 8), :] = (up + down) + (mid + mid)
             return carry
 
         lax.fori_loop(0, groups + 1, body, 0)
 
     def column_stage(t):
+        size = (BLOCK * tall, LANES)
+        lane = lax.broadcasted_iota(jnp.int32, size, 1)
         left_edge, right_edge = (lane == 0, lane == LANES - 1)
         left_half = lane >= LANES // 2
         low = jnp.where(t == 0, -BIG, BIG)
         high = jnp.where(t == tiles - 1, -BIG, BIG)
         bound = jnp.where(left_half, low, high)
 
-        def body(k, carry):
-            at = pl.ds(pl.multiple_of(8 * k, 8), 8)
+        def body(m, carry):
+            at = pl.ds(pl.multiple_of(m * (BLOCK * tall), 8), BLOCK * tall)
+            middle = second[t + 1, at, :]
+            whole = jnp.concatenate([middle, jnp.where(left_half, second[t, at, :], second[t + 2, at, :])], axis=1)
+            upper = whole.astype(jnp.bfloat16)
+            lower = (whole - upper.astype(jnp.float32)).astype(jnp.bfloat16)
+            out = jnp.dot(upper, mix[...], preferred_element_type=jnp.float32) + jnp.dot(lower, mix[...], preferred_element_type=jnp.float32)
+            value = out[:, 0:LANES]
+            beside = jnp.minimum(out[:, LANES:], bound)
+            from_left = pltpu.roll(jnp.where(right_edge, beside, value), 1, 1)
+            from_right = pltpu.roll(jnp.where(left_edge, beside, value), LANES - 1, 1)
+            wide[at, :] = jnp.maximum(jnp.maximum(from_left, from_right), value)
+            smooth[at, :] = value
+            return carry
+
+        lax.fori_loop(0, planes // BLOCK, body, 0)
+
+        @pl.when(jnp.logical_not(has_upper))
+        def _():
             for i in range(planes):
-                a, b, c = (second[i, t, at, :], second[i, t + 1, at, :], second[i, t + 2, at, :])
-                w = jnp.where(left_half, a, c)
-                to_right = pltpu.roll(jnp.where(right_edge, a, b), 1, 1)
-                to_left = pltpu.roll(jnp.where(left_edge, c, b), LANES - 1, 1)
-                value = (to_right + to_left) + (b + b)
-                w_right = pltpu.roll(jnp.where(right_edge, b, w), 1, 1)
-                w_left = pltpu.roll(jnp.where(left_edge, b, w), LANES - 1, 1)
-                beside = jnp.minimum((w_right + w_left) + (w + w), bound)
-                from_left = pltpu.roll(jnp.where(right_edge, beside, value), 1, 1)
-                from_right = pltpu.roll(jnp.where(left_edge, beside, value), LANES - 1, 1)
-                wide[i, at, :] = jnp.maximum(jnp.maximum(from_left, from_right), value)
-                if 0 < i < planes - 1:
-                    smooth[i - 1, at, :] = value
-            return carry
-
-        lax.fori_loop(0, groups + 1, body, 0)
-
-        @pl.when(jnp.logical_not(has_upper))
+                wide[i * tall : i * tall + 1, :] = jnp.full((1, LANES), -BIG)
+
+        @pl.when(jnp.logical_not(has_lower))
         def _():
             for i in range(planes):
-                wide[i, 0:1, :] = jnp.full((1, LANES), -BIG)
-
-        @pl.when(jnp.logical_not(has_lower))
-        def _():
-            for i in range(planes):
-                wide[i, rows + 1 : rows + 2, :] = jnp.full((1, LANES), -BIG)
+                wide[i * tall + rows + 1 : i * tall + rows + 2, :] = jnp.full((1, LANES), -BIG)
 
     def weight_stage(t):
         def body(g, carry):
             start = pl.multiple_of(8 * g, 8)
             limit = level[pl.ds(start, 8), :]
-            tall = []
+            columns = []
             for i in range(planes):
-                up = wide[i, pl.ds(8 * g, 8), :]
-                mid = wide[i, pl.ds(8 * g + 1, 8), :]
-                down = wide[i, pl.ds(8 * g + 2, 8), :]
-                tall.append(jnp.maximum(jnp.maximum(up, down), mid))
+                up = wide[pl.ds(i * tall + 8 * g, 8), :]
+                mid = wide[pl.ds(i * tall + 8 * g + 1, 8), :]
+                down = wide[pl.ds(i * tall + 8 * g + 2, 8), :]
+                columns.append(jnp.maximum(jnp.maximum(up, down), mid))
                 if i >= 2:
-                    highest = jnp.maximum(jnp.maximum(tall[i - 2], tall[i - 1]), tall[i])
-                    value = smooth[i - 2, pl.ds(8 * g + 1, 8), :]
+                    highest = jnp.maximum(jnp.maximum(columns[i - 2], columns[i - 1]), columns[i])
+                    value = smooth[pl.ds((i - 1) * tall + 8 * g + 1, 8), :]
                     sharp = jnp.exp2((value - highest) * (SHARP * LOG2E / 64.0))
                     weight[i - 2, t, pl.ds(start, 8), :] = sharp * (jnp.maximum(value - limit, 0.0) * (1.0 / 64.0))
             return carry
@@ -178,8 +201,16 @@
         column_stage(t)
         weight_stage(t)
 
-    for chunk in range(DEPTH):
+    issue(0)
+    for t in range(tiles):
+        load(1, t).wait()
+    issue(1)
+    for t in range(tiles):
+        load(2, t).wait()
+    for chunk in range(2, DEPTH):
         issue(chunk)
+
+    prepare()
 
     def edge(side):
         arrive(side)
@@ -352,14 +383,15 @@
             pltpu.SMEM((rows,), jnp.int32),
             pltpu.VMEM((depth + 2 * REACH, tiles, rows, LANES), jnp.float32),
             pltpu.VMEM((planes, tiles, rows + 16, LANES), jnp.float32),
-            pltpu.VMEM((planes, tiles + 2, rows + 8, LANES), jnp.float32),
-            pltpu.VMEM((depth, rows + 8, LANES), jnp.float32),
-            pltpu.VMEM((planes, rows + 8, LANES), jnp.float32),
+            pltpu.VMEM((tiles + 2, planes * (rows + 8), LANES), jnp.float32),
+            pltpu.VMEM((planes * (rows + 8), LANES), jnp.float32),
+            pltpu.VMEM((planes * (rows + 8), LANES), jnp.float32),
             pltpu.VMEM((rows, LANES), jnp.float32),
+            pltpu.VMEM((2 * LANES, 2 * LANES), jnp.bfloat16),
             pltpu.VMEM((2, planes * tiles * 2, LANES), jnp.float32),
             pltpu.VMEM((2, planes * tiles * 2, LANES), jnp.float32),
             pltpu.SemaphoreType.DMA,
-            pltpu.SemaphoreType.DMA((tiles,)),
+            pltpu.SemaphoreType.DMA((3, tiles)),
             pltpu.SemaphoreType.DMA((2, tiles + 2)),
             pltpu.SemaphoreType.DMA((2, tiles + 2)),
             pltpu.SemaphoreType.DMA((2,)),

time: 72.1 us -> 57.5 us (0.80)
  Pallas kernels: 71.4 us -> 56.8 us
    pallas_call x1, Pallas kernels: 68.2 us -> 53.5 us  [on_device(): pl.pallas_call(functools.partial(spread_kernel, n_omega, n_row), out_shap...]
where the time goes in v3:
time: 57.5 us; the launch traced here: 57.4 us
  Pallas kernels  56.8 us (99%)
  between operations  0.65 us (1%)
    pallas_call x1, Pallas kernels, on_device(): pl.pallas_call(functools.partial(spread_kernel, n_omega, n_row), out_shap...  53.5 us
    pallas_call x1, Pallas kernels, on_device(): pl.pallas_call(moments_kernel, out_shape=(jax.ShapeDtypeStruct(frames.sha...  3.21 us

profile of v3, /device:TPU:1, one launch (start us, length us, event | category | flops | bytes accessed | tf_op | source)
XLA Modules:
  0.0 57.4 jit_solution(1161268079709668458)
XLA Ops:
  0.6 0.0 copy-start
  0.6 53.5 %spread.1.weight = f32[16,8,64,128]{3,2,1,0:T(8,128)S(1)} custom-call(f32[16,64,1024]{2,1,0:T(8,128)} %frames.1, s32[64]{0:T(128)} %limits.1), custom_call_target="tpu_custom_call" | custom-call | tf_op jit(solution)/shard_map/spread/pallas_call | solution.py:377
  54.2 0.0 copy-done
  54.2 3.2 %moments.1 = (f32[16,64,1024]{2,1,0:T(8,128)}, f32[4,32]{1,0:T(4,128)}) custom-call(s32[3,32]{1,0:T(4,128)S(1)} %copy-done, f32[16,8,64,128]{3,2,1,0:T(8,128)S(1)} %spread.1.weight), custom_call_target="tpu_custom_call" | custom-call | tf_op jit(solution)/shard_map/moments/pallas_call | solution.py:403
Async XLA Ops:
  0.6 53.6 %copy-start = (s32[3,32]{1,0:T(4,128)S(1)}, s32[3,32]{1,0:T(4,128)}, u32[]{:S(2)}) copy-start(s32[3,32]{1,0:T(4,128)} %boxes.1) | copy-start | bytes 1156

commit v4 on v3

--- a/solution.py
+++ b/solution.py
@@ -16,120 +16,19 @@
 LOG2E = 1.4426950408889634
 BIG = 3.0e38
 LANES = 128
-DEPTH = 3
+NEAR, FAR = (3, 1)
 LATE = 1
-BLOCK = 6
+BLOCK = 18
 MESH = pl.DeviceIdType.MESH
 
 
-def spread_kernel(n_omega, n_row, frames, limits, weight, thresholds, x, first, second, smooth, wide, level, mix, outgoing, incoming, limit_sem, load_sem, send_sem, recv_sem, row_send, row_recv):
-    depth, rows = (frames.shape[0], frames.shape[1])
-    tiles = frames.shape[2] // LANES
+def stages(n_row, first, second, smooth, wide, level, mix, weight):
+    planes, tiles = (first.shape[0], first.shape[1])
+    rows = level.shape[0]
     groups = rows // 8
-    planes = depth + 2
     tall = rows + 8
-    omega, row = (lax.axis_index("omega"), lax.axis_index("row"))
-    after, before = (lax.rem(omega + 1, n_omega), lax.rem(omega + n_omega - 1, n_omega))
+    row = lax.axis_index("row")
     has_upper, has_lower = (row > 0, row < n_row - 1)
-
-    def load(part, t):
-        start, count = ((0, 8), (rows - 8, 8), (8, rows - 16))[part]
-        return pltpu.make_async_copy(
-            frames.at[:, pl.ds(start, count), pl.ds(t * LANES, LANES)], x.at[pl.ds(REACH, depth), t, pl.ds(start, count), :], load_sem.at[part, t]
-        )
-
-    limits_copy = pltpu.make_async_copy(limits, thresholds, limit_sem)
-    for part in range(3):
-        for t in range(tiles):
-            load(part, t).start()
-    limits_copy.start()
-
-    barrier = pltpu.get_barrier_semaphore()
-    for neighbour in (before, after):
-        pl.semaphore_signal(barrier, inc=1, device_id=(neighbour, row), device_id_type=MESH)
-
-    @pl.when(has_upper)
-    def _():
-        pl.semaphore_signal(barrier, inc=1, device_id=(omega, row - 1), device_id_type=MESH)
-
-    @pl.when(has_lower)
-    def _():
-        pl.semaphore_signal(barrier, inc=1, device_id=(omega, row + 1), device_id_type=MESH)
-
-    sub = lax.broadcasted_iota(jnp.int32, (8, LANES), 0)
-
-    def prepare():
-        limits_copy.wait()
-        for g in range(groups):
-            tile = jnp.full((8, LANES), thresholds[g * 8].astype(jnp.float32))
-            for j in range(1, 8):
-                tile = jnp.where(sub == j, thresholds[g * 8 + j].astype(jnp.float32), tile)
-            level[g * 8 : g * 8 + 8, :] = tile
-        blank = jnp.zeros((tall, LANES), jnp.float32)
-        for i in range(planes):
-            second[0, i * tall : (i + 1) * tall, :] = blank
-            second[tiles + 1, i * tall : (i + 1) * tall, :] = blank
-        last = LANES - 1
-        size = (LANES, LANES)
-        source, place = (lax.broadcasted_iota(jnp.int32, size, 0), lax.broadcasted_iota(jnp.int32, size, 1))
-
-        def taps(pairs):
-            total = jnp.zeros(size, jnp.float32)
-            for test, value in pairs:
-                total = total + jnp.where(test, value, 0.0)
-            return total.astype(jnp.bfloat16)
-
-        at_first, at_last = (place == 0, place == last)
-        mix[0:LANES, 0:LANES] = taps([(source == place, 2.0), (source == place - 1, 1.0), (source == place + 1, 1.0)])
-        mix[LANES:, 0:LANES] = taps([(at_first & (source == last), 1.0), (at_last & (source == 0), 1.0)])
-        mix[0:LANES, LANES:] = taps([(at_first & (source == last), 1.0), (at_last & (source == 0), 1.0)])
-        mix[LANES:, LANES:] = taps(
-            [(at_first & (source == 0), 2.0), (at_first & (source == 1), 1.0), (at_last & (source == last), 2.0), (at_last & (source == last - 1), 1.0)]
-        )
-
-    def piece(start, chunk):
-        planes_of = pl.ds(start, REACH)
-        if isinstance(chunk, int) and chunk < 2:
-            return x.at[planes_of, :, pl.ds(0 if chunk == 0 else rows - 8, 8), :]
-        return x.at[planes_of, chunk - 2, pl.ds(8, rows - 16), :]
-
-    def copies(chunk):
-        to_before = pltpu.make_async_remote_copy(
-            src_ref=piece(REACH, chunk), dst_ref=piece(REACH + depth, chunk), send_sem=send_sem.at[0, chunk], recv_sem=recv_sem.at[0, chunk], device_id=(before, row), device_id_type=MESH
-        )
-        to_after = pltpu.make_async_remote_copy(
-            src_ref=piece(depth, chunk), dst_ref=piece(0, chunk), send_sem=send_sem.at[1, chunk], recv_sem=recv_sem.at[1, chunk], device_id=(after, row), device_id_type=MESH
-        )
-        return (to_before, to_after)
-
-    def row_copy(side):
-        return pltpu.make_async_remote_copy(
-            src_ref=outgoing.at[side], dst_ref=incoming.at[side], send_sem=row_send.at[side], recv_sem=row_recv.at[side], device_id=(omega, row - 1 if side == 0 else row + 1), device_id_type=MESH
-        )
-
-    for t in range(tiles):
-        load(0, t).wait()
-    pl.semaphore_wait(barrier, 2 + has_upper.astype(jnp.int32) + has_lower.astype(jnp.int32))
-
-    def issue(chunk):
-        for copy in copies(chunk):
-            copy.start()
-
-    def arrive(chunk):
-        for copy in copies(chunk):
-            copy.wait_recv()
-        for copy in copies(chunk):
-            copy.wait_send()
-
-    def frame_stage(t, start):
-        v = [x[j, t, pl.ds(start, 8), :] for j in range(depth + 2 * REACH)]
-        s2 = [v[j] + v[j + 1] for j in range(len(v) - 1)]
-        s4 = [s2[j] + s2[j + 2] for j in range(len(s2) - 2)]
-        s8 = [s4[j] + s4[j + 4] for j in range(len(s4) - 4)]
-        c = [v[j + BW] - (s8[j] + v[j + 2 * BW]) * (1.0 / (2 * BW + 1)) for j in range(depth + 4)]
-        p = [c[j] + c[j + 1] for j in range(depth + 3)]
-        for i in range(planes):
-            first[i, t, pl.ds(start + 8, 8), :] = p[i] + p[i + 1]
 
     def row_stage(t):
         def body(k, carry):
@@ -201,20 +100,158 @@
         column_stage(t)
         weight_stage(t)
 
+    return (row_stage, finish)
+
+
+def spread_kernel(n_omega, n_row, frames, limits, weight, first, second, level, mix, thresholds, x, smooth, wide, outgoing, incoming, limit_sem, load_sem, send_sem, recv_sem, row_send, row_recv):
+    depth, rows = (frames.shape[0], frames.shape[1])
+    tiles = frames.shape[2] // LANES
+    groups = rows // 8
+    planes = depth + 2
+    tall = rows + 8
+    omega, row = (lax.axis_index("omega"), lax.axis_index("row"))
+    after, before = (lax.rem(omega + 1, n_omega), lax.rem(omega + n_omega - 1, n_omega))
+    has_upper, has_lower = (row > 0, row < n_row - 1)
+
+    def load(part, t):
+        start, count = ((0, 8), (rows - 8, 8), (8, rows - 16))[part]
+        return pltpu.make_async_copy(
+            frames.at[:, pl.ds(start, count), pl.ds(t * LANES, LANES)], x.at[pl.ds(REACH, depth), t, pl.ds(start, count), :], load_sem.at[part, t]
+        )
+
+    limits_copy = pltpu.make_async_copy(limits, thresholds, limit_sem)
+    for part in range(3):
+        for t in range(tiles):
+            load(part, t).start()
+    limits_copy.start()
+
+    barrier = pltpu.get_barrier_semaphore()
+    for neighbour in (before, after):
+        pl.semaphore_signal(barrier, inc=1, device_id=(neighbour, row), device_id_type=MESH)
+
+    @pl.when(has_upper)
+    def _():
+        pl.semaphore_signal(barrier, inc=1, device_id=(omega, row - 1), device_id_type=MESH)
+
+    @pl.when(has_lower)
+    def _():
+        pl.semaphore_signal(barrier, inc=1, device_id=(omega, row + 1), device_id_type=MESH)
+
+    sub = lax.broadcasted_iota(jnp.int32, (8, LANES), 0)
+
+    def prepare():
+        limits_copy.wait()
+        for g in range(groups):
+            tile = jnp.full((8, LANES), thresholds[g * 8].astype(jnp.float32))
+            for j in range(1, 8):
+                tile = jnp.where(sub == j, thresholds[g * 8 + j].astype(jnp.float32), tile)
+            level[g * 8 : g * 8 + 8, :] = tile
+        blank = jnp.zeros((tall, LANES), jnp.float32)
+        for i in range(planes):
+            second[0, i * tall : (i + 1) * tall, :] = blank
+            second[tiles + 1, i * tall : (i + 1) * tall, :] = blank
+        last = LANES - 1
+        size = (LANES, LANES)
+        source, place = (lax.broadcasted_iota(jnp.int32, size, 0), lax.broadcasted_iota(jnp.int32, size, 1))
+
+        def taps(pairs):
+            total = jnp.zeros(size, jnp.float32)
+            for test, value in pairs:
+                total = total + jnp.where(test, value, 0.0)
+            return total.astype(jnp.bfloat16)
+
+        at_first, at_last = (place == 0, place == last)
+        mix[0:LANES, 0:LANES] = taps([(source == place, 2.0), (source == place - 1, 1.0), (source == place + 1, 1.0)])
+        mix[LANES:, 0:LANES] = taps([(at_first & (source == last), 1.0), (at_last & (source == 0), 1.0)])
+        mix[0:LANES, LANES:] = taps([(at_first & (source == last), 1.0), (at_last & (source == 0), 1.0)])
+        mix[LANES:, LANES:] = taps(
+            [(at_first & (source == 0), 2.0), (at_first & (source == 1), 1.0), (at_last & (source == last), 2.0), (at_last & (source == last - 1), 1.0)]
+        )
+
+    def piece(start, chunk):
+        planes_of = pl.ds(start, REACH)
+        if isinstance(chunk, int) and chunk < 2:
+            return x.at[planes_of, :, pl.ds(0 if chunk == 0 else rows - 8, 8), :]
+        return x.at[planes_of, chunk - 2, pl.ds(8, rows - 16), :]
+
+    def copies(chunk):
+        to_before = pltpu.make_async_remote_copy(
+            src_ref=piece(REACH, chunk), dst_ref=piece(REACH + depth, chunk), send_sem=send_sem.at[0, chunk], recv_sem=recv_sem.at[0, chunk], device_id=(before, row), device_id_type=MESH
+        )
+        to_after = pltpu.make_async_remote_copy(
+            src_ref=piece(depth, chunk), dst_ref=piece(0, chunk), send_sem=send_sem.at[1, chunk], recv_sem=recv_sem.at[1, chunk], device_id=(after, row), device_id_type=MESH
+        )
+        return (to_before, to_after)
+
+    def row_copy(side):
+        return pltpu.make_async_remote_copy(
+            src_ref=outgoing.at[side], dst_ref=incoming.at[side], send_sem=row_send.at[side], recv_sem=row_recv.at[side], device_id=(omega, row - 1 if side == 0 else row + 1), device_id_type=MESH
+        )
+
+    for t in range(tiles):
+        load(0, t).wait()
+    pl.semaphore_wait(barrier, 2 + has_upper.astype(jnp.int32) + has_lower.astype(jnp.int32))
+
+    def issue(chunk):
+        for copy in copies(chunk):
+            copy.start()
+
+    corner = lax.rem(omega, 4)
+    ahead = jnp.where((corner == 0) | (corner == 3), FAR, NEAR)
+
+    def sent(chunk):
+        for copy in copies(chunk):
+            copy.wait_send()
+
+    def arrive(chunk):
+        for copy in copies(chunk):
+            copy.wait_recv()
+
+    def frame_stage(t, start):
+        v = [x[j, t, pl.ds(start, 8), :] for j in range(depth + 2 * REACH)]
+        s2 = [v[j] + v[j + 1] for j in range(len(v) - 1)]
+        s4 = [s2[j] + s2[j + 2] for j in range(len(s2) - 2)]
+        s8 = [s4[j] + s4[j + 4] for j in range(len(s4) - 4)]
+        c = [v[j + BW] - (s8[j] + v[j + 2 * BW]) * (1.0 / (2 * BW + 1)) for j in range(depth + 4)]
+        p = [c[j] + c[j + 1] for j in range(depth + 3)]
+        for i in range(planes):
+            first[i, t, pl.ds(start + 8, 8), :] = p[i] + p[i + 1]
+
+    row_stage, finish = stages(n_row, first, second, smooth, wide, level, mix, weight)
+
     issue(0)
     for t in range(tiles):
         load(1, t).wait()
-    issue(1)
+
+    @pl.when(ahead >= 2)
+    def _():
+        issue(1)
+
     for t in range(tiles):
         load(2, t).wait()
-    for chunk in range(2, DEPTH):
-        issue(chunk)
+    for chunk in range(2, max(NEAR, FAR)):
+
+        @pl.when(ahead > chunk)
+        def _():
+            issue(chunk)
 
     prepare()
 
     def edge(side):
+        sent(side)
+        if side == 0 and min(NEAR, FAR) == 1:
+
+            @pl.when(ahead == 1)
+            def _():
+                issue(1)
+
+            @pl.when(ahead > 1)
+            def _():
+                issue(ahead)
+
+        else:
+            issue(ahead + side)
         arrive(side)
-        issue(side + DEPTH)
         start = 0 if side == 0 else rows - 8
 
         def body(t, carry):
@@ -233,11 +270,13 @@
     edge(1)
 
     def take(t):
+        sent(t + 2)
+
+        @pl.when(t + 2 + ahead < tiles + 2)
+        def _():
+            issue(t + 2 + ahead)
+
         arrive(t + 2)
-
-        @pl.when(t + 2 + DEPTH < tiles + 2)
-        def _():
-            issue(t + 2 + DEPTH)
 
         def body(g, carry):
             frame_stage(t, pl.multiple_of(8 * g, 8))
@@ -290,8 +329,8 @@
         finish(t - 1)
         return carry
 
-    lax.fori_loop(LATE + 1, tiles, late, 0)
-    finish(tiles - 1)
+    lax.fori_loop(LATE + 1, tiles - 1, late, 0)
+    take(tiles - 1)
 
     for side in range(2):
 
@@ -300,15 +339,24 @@
             row_copy(side).wait_send()
 
 
-def moments_kernel(boxes, weight, out, moments, parts, sem):
+def moments_kernel(n_row, boxes, first, second_in, level, mix, weight_in, out, moments, second, weight, smooth, wide, parts, sem):
     depth, tiles, rows = weight.shape[0:3]
     slots = boxes.shape[1]
 
     def store(t):
         return pltpu.make_async_copy(weight.at[:, t], out.at[:, :, pl.ds(t * LANES, LANES)], sem.at[t])
 
-    for t in range(tiles):
+    for t in range(tiles - 2):
         store(t).start()
+    row_stage, finish = stages(n_row, first, second, smooth, wide, level, mix, weight)
+    row_stage(tiles - 1)
+
+    def tail(t, carry):
+        finish(t)
+        store(t).start()
+        return carry
+
+    lax.fori_loop(tiles - 2, tiles, tail, 0)
     frame_base = lax.axis_index("omega") * depth
     row_base = lax.axis_index("row") * rows
     sub = lax.broadcasted_iota(jnp.int32, (8, LANES), 0)
@@ -374,20 +422,24 @@
     vmem = functools.partial(pl.BlockSpec, memory_space=pltpu.VMEM)
     smem = functools.partial(pl.BlockSpec, memory_space=pltpu.SMEM)
     anywhere = functools.partial(pl.BlockSpec, memory_space=pl.ANY)
-    weight = pl.pallas_call(
+    tall = planes * (rows + 8)
+    kept = (
+        pltpu.VMEM((depth, tiles, rows, LANES), jnp.float32),
+        pltpu.VMEM((planes, tiles, rows + 16, LANES), jnp.float32),
+        pltpu.VMEM((tiles + 2, tall, LANES), jnp.float32),
+        pltpu.VMEM((rows, LANES), jnp.float32),
+        pltpu.VMEM((2 * LANES, 2 * LANES), jnp.bfloat16),
+    )
+    weight, first, second, level, mix = pl.pallas_call(
         functools.partial(spread_kernel, n_omega, n_row),
-        out_shape=pltpu.VMEM((depth, tiles, rows, LANES), jnp.float32),
+        out_shape=kept,
         in_specs=[pl.BlockSpec(memory_space=pltpu.HBM), pl.BlockSpec(memory_space=pltpu.HBM)],
-        out_specs=vmem(),
+        out_specs=tuple(vmem() for _ in kept),
         scratch_shapes=[
             pltpu.SMEM((rows,), jnp.int32),
             pltpu.VMEM((depth + 2 * REACH, tiles, rows, LANES), jnp.float32),
-            pltpu.VMEM((planes, tiles, rows + 16, LANES), jnp.float32),
-            pltpu.VMEM((tiles + 2, planes * (rows + 8), LANES), jnp.float32),
-            pltpu.VMEM((planes * (rows + 8), LANES), jnp.float32),
-            pltpu.VMEM((planes * (rows + 8), LANES), jnp.float32),
-            pltpu.VMEM((rows, LANES), jnp.float32),
-            pltpu.VMEM((2 * LANES, 2 * LANES), jnp.bfloat16),
+            pltpu.VMEM((tall, LANES), jnp.float32),
+            pltpu.VMEM((tall, LANES), jnp.float32),
             pltpu.VMEM((2, planes * tiles * 2, LANES), jnp.float32),
             pltpu.VMEM((2, planes * tiles * 2, LANES), jnp.float32),
             pltpu.SemaphoreType.DMA,
@@ -397,18 +449,25 @@
             pltpu.SemaphoreType.DMA((2,)),
             pltpu.SemaphoreType.DMA((2,)),
         ],
-        compiler_params=pltpu.CompilerParams(collective_id=0, has_side_effects=True, vmem_limit_bytes=54 << 20),
+        compiler_params=pltpu.CompilerParams(collective_id=0, has_side_effects=True, vmem_limit_bytes=40 << 20),
         name="spread",
     )(frames, thresholds)
-    return pl.pallas_call(
-        moments_kernel,
-        out_shape=(jax.ShapeDtypeStruct(frames.shape, jnp.float32), jax.ShapeDtypeStruct((4, slots), jnp.float32)),
-        in_specs=[smem(), vmem()],
-        out_specs=(anywhere(), vmem()),
-        scratch_shapes=[pltpu.VMEM((4, slots * 8, LANES), jnp.float32), pltpu.SemaphoreType.DMA((tiles,))],
+    out = pl.pallas_call(
+        functools.partial(moments_kernel, n_row),
+        out_shape=(jax.ShapeDtypeStruct(frames.shape, jnp.float32), jax.ShapeDtypeStruct((4, slots), jnp.float32), kept[2], kept[0]),
+        in_specs=[smem(), vmem(), vmem(), vmem(), vmem(), vmem()],
+        out_specs=(anywhere(), vmem(), vmem(), vmem()),
+        scratch_shapes=[
+            pltpu.VMEM((tall, LANES), jnp.float32),
+            pltpu.VMEM((tall, LANES), jnp.float32),
+            pltpu.VMEM((4, slots * 8, LANES), jnp.float32),
+            pltpu.SemaphoreType.DMA((tiles,)),
+        ],
+        input_output_aliases={2: 2, 5: 3},
         compiler_params=pltpu.CompilerParams(vmem_limit_bytes=8 << 20),
         name="moments",
-    )(spot_boxes, weight)
+    )(spot_boxes, first, second, level, mix, weight)
+    return out[0:2]
 
 
 def solution(mesh):

time: 57.5 us -> 54 us (0.939)
  Pallas kernels: 56.8 us -> 53.1 us
    pallas_call x1, Pallas kernels: 53.5 us -> 48.8 us  [on_device(): pl.pallas_call(functools.partial(spread_kernel, n_omega, n_row), out_shap...]
    pallas_call x1, Pallas kernels: 3.21 us -> 4.28 us  [on_device(): pl.pallas_call(functools.partial(moments_kernel, n_row), out_shape=(jax.S...]
where the time goes in v4:
time: 54 us; the launch traced here: 53.8 us
  Pallas kernels  53.1 us (98%)
  between operations  0.65 us (1%)
    pallas_call x1, Pallas kernels, on_device(): pl.pallas_call(functools.partial(spread_kernel, n_omega, n_row), out_shap...  48.8 us
    pallas_call x1, Pallas kernels, on_device(): pl.pallas_call(functools.partial(moments_kernel, n_row), out_shape=(jax.S...  4.28 us

profile of v4, /device:TPU:1, one launch (start us, length us, event | category | flops | bytes accessed | tf_op | source)
XLA Modules:
  0.0 53.8 jit_solution(17870368272850046473)
XLA Ops:
  0.6 0.0 copy-start
  0.6 48.8 %spread.1 = (f32[16,8,64,128]{3,2,1,0:T(8,128)S(1)}, f32[18,8,80,128]{3,2,1,0:T(8,128)S(1)}, f32[10,1296,128]{2,1,0:T(8,128)S(1)}, f32[64,128]{1,0:T(8,128)S(1)}, bf16[256,256]{1,0:T(8,128)(2,1)S(1)}) custom-call(f32[16,64,1024]{2,1,0:T(8,128)} %frames.1, s32[64]{0:T(128)} %limits.1), custom_call_target="tpu_custom_call" | custom-call | tf_op jit(solution)/shard_map/spread/pallas_call | solution.py:433
  49.5 0.0 copy-done
  49.5 4.3 %moments.1 = (f32[16,64,1024]{2,1,0:T(8,128)}, f32[4,32]{1,0:T(4,128)}, f32[10,1296,128]{2,1,0:T(8,128)S(1)}, f32[16,8,64,128]{3,2,1,0:T(8,128)S(1)}) custom-call(s32[3,32]{1,0:T(4,128)S(1)} %copy-done, f32[18,8,80,128]{3,2,1,0:T(8,128)S(1)} %get-tuple-element.9.first, ...), custom_call_target="tpu_custom_call", output_to_operand_aliasing={{2}: (2, {}), {3}: (5, {})} | custom-call | tf_op jit(solution)/shard_map/moments/pallas_call | solution.py:455
Async XLA Ops:
  0.6 48.9 %copy-start = (s32[3,32]{1,0:T(4,128)S(1)}, s32[3,32]{1,0:T(4,128)}, u32[]{:S(2)}) copy-start(s32[3,32]{1,0:T(4,128)} %boxes.1) | copy-start | bytes 1156

commit v5 on v4

--- a/solution.py
+++ b/solution.py
@@ -19,6 +19,7 @@
 NEAR, FAR = (3, 1)
 LATE = 1
 BLOCK = 18
+ROW_STEP = 3
 MESH = pl.DeviceIdType.MESH
 
 
@@ -31,15 +32,17 @@
     has_upper, has_lower = (row > 0, row < n_row - 1)
 
     def row_stage(t):
-        def body(k, carry):
-            for i in range(planes):
-                up = first[i, t, pl.ds(8 * k + 6, 8), :]
-                mid = first[i, t, pl.ds(8 * k + 7, 8), :]
-                down = first[i, t, pl.ds(8 * k + 8, 8), :]
-                second[t + 1, pl.ds(pl.multiple_of(i * tall + 8 * k, 8), 8), :] = (up + down) + (mid + mid)
+        def body(step, carry):
+            for j in range(ROW_STEP):
+                k = step * ROW_STEP + j
+                for i in range(planes):
+                    up = first[i, t, pl.ds(8 * k + 6, 8), :]
+                    mid = first[i, t, pl.ds(8 * k + 7, 8), :]
+                    down = first[i, t, pl.ds(8 * k + 8, 8), :]
+                    second[t + 1, pl.ds(pl.multiple_of(i * tall + 8 * k, 8), 8), :] = (up + down) + (mid + mid)
             return carry
 
-        lax.fori_loop(0, groups + 1, body, 0)
+        lax.fori_loop(0, (groups + 1) // ROW_STEP, body, 0)
 
     def column_stage(t):
         size = (BLOCK * tall, LANES)
@@ -78,7 +81,7 @@
                 wide[i * tall + rows + 1 : i * tall + rows + 2, :] = jnp.full((1, LANES), -BIG)
 
     def weight_stage(t):
-        def body(g, carry):
+        def group(g):
             start = pl.multiple_of(8 * g, 8)
             limit = level[pl.ds(start, 8), :]
             columns = []
@@ -92,9 +95,13 @@
                     value = smooth[pl.ds((i - 1) * tall + 8 * g + 1, 8), :]
                     sharp = jnp.exp2((value - highest) * (SHARP * LOG2E / 64.0))
                     weight[i - 2, t, pl.ds(start, 8), :] = sharp * (jnp.maximum(value - limit, 0.0) * (1.0 / 64.0))
+
+        def body(step, carry):
+            for j in range(2):
+                group(step * 2 + j)
             return carry
 
-        lax.fori_loop(0, groups, body, 0)
+        lax.fori_loop(0, groups // 2, body, 0)
 
     def finish(t):
         column_stage(t)
@@ -119,23 +126,23 @@
             frames.at[:, pl.ds(start, count), pl.ds(t * LANES, LANES)], x.at[pl.ds(REACH, depth), t, pl.ds(start, count), :], load_sem.at[part, t]
         )
 
+    barrier = pltpu.get_barrier_semaphore()
+    for neighbour in (before, after):
+        pl.semaphore_signal(barrier, inc=1, device_id=(neighbour, row), device_id_type=MESH)
+
+    @pl.when(has_upper)
+    def _():
+        pl.semaphore_signal(barrier, inc=1, device_id=(omega, row - 1), device_id_type=MESH)
+
+    @pl.when(has_lower)
+    def _():
+        pl.semaphore_signal(barrier, inc=1, device_id=(omega, row + 1), device_id_type=MESH)
+
     limits_copy = pltpu.make_async_copy(limits, thresholds, limit_sem)
     for part in range(3):
         for t in range(tiles):
             load(part, t).start()
     limits_copy.start()
-
-    barrier = pltpu.get_barrier_semaphore()
-    for neighbour in (before, after):
-        pl.semaphore_signal(barrier, inc=1, device_id=(neighbour, row), device_id_type=MESH)
-
-    @pl.when(has_upper)
-    def _():
-        pl.semaphore_signal(barrier, inc=1, device_id=(omega, row - 1), device_id_type=MESH)
-
-    @pl.when(has_lower)
-    def _():
-        pl.semaphore_signal(barrier, inc=1, device_id=(omega, row + 1), device_id_type=MESH)
 
     sub = lax.broadcasted_iota(jnp.int32, (8, LANES), 0)
 
@@ -278,11 +285,12 @@
 
         arrive(t + 2)
 
-        def body(g, carry):
-            frame_stage(t, pl.multiple_of(8 * g, 8))
+        def body(step, carry):
+            for j in range(2):
+                frame_stage(t, pl.multiple_of(8 * (step * 2 + j + 1), 8))
             return carry
 
-        lax.fori_loop(1, groups - 1, body, 0)
+        lax.fori_loop(0, (groups - 2) // 2, body, 0)
 
     def early(t, carry):
         take(t)

time: 54 us -> 53.7 us (level)
  no operation moved by 1% of the time
where the time goes in v5:
time: 53.7 us
  Pallas kernels  53 us (99%)
  between operations  0.65 us (1%)
    pallas_call x1, Pallas kernels, on_device(): pl.pallas_call(functools.partial(spread_kernel, n_omega, n_row), out_shap...  48.8 us
    pallas_call x1, Pallas kernels, on_device(): pl.pallas_call(functools.partial(moments_kernel, n_row), out_shape=(jax.S...  4.27 us

profile of v5, /device:TPU:1, one launch (start us, length us, event | category | flops | bytes accessed | tf_op | source)
XLA Modules:
  0.0 53.7 jit_solution(798064041040986863)
XLA Ops:
  0.6 0.0 copy-start
  0.6 48.8 %spread.1 = (f32[16,8,64,128]{3,2,1,0:T(8,128)S(1)}, f32[18,8,80,128]{3,2,1,0:T(8,128)S(1)}, f32[10,1296,128]{2,1,0:T(8,128)S(1)}, f32[64,128]{1,0:T(8,128)S(1)}, bf16[256,256]{1,0:T(8,128)(2,1)S(1)}) custom-call(f32[16,64,1024]{2,1,0:T(8,128)} %frames.1, s32[64]{0:T(128)} %limits.1), custom_call_target="tpu_custom_call" | custom-call | tf_op jit(solution)/shard_map/spread/pallas_call | solution.py:441
  49.4 0.0 copy-done
  49.4 4.3 %moments.1 = (f32[16,64,1024]{2,1,0:T(8,128)}, f32[4,32]{1,0:T(4,128)}, f32[10,1296,128]{2,1,0:T(8,128)S(1)}, f32[16,8,64,128]{3,2,1,0:T(8,128)S(1)}) custom-call(s32[3,32]{1,0:T(4,128)S(1)} %copy-done, f32[18,8,80,128]{3,2,1,0:T(8,128)S(1)} %get-tuple-element.9.first, ...), custom_call_target="tpu_custom_call", output_to_operand_aliasing={{2}: (2, {}), {3}: (5, {})} | custom-call | tf_op jit(solution)/shard_map/moments/pallas_call | solution.py:463
Async XLA Ops:
  0.6 48.8 %copy-start = (s32[3,32]{1,0:T(4,128)S(1)}, s32[3,32]{1,0:T(4,128)}, u32[]{:S(2)}) copy-start(s32[3,32]{1,0:T(4,128)} %boxes.1) | copy-start | bytes 1156

commit v6 on v5

--- a/solution.py
+++ b/solution.py
@@ -68,8 +68,10 @@
             smooth[at, :] = value
             return carry
 
-        lax.fori_loop(0, planes // BLOCK, body, 0)
-
+        for m in range(planes // BLOCK):
+            body(m, 0)
+
+    def outside():
         @pl.when(jnp.logical_not(has_upper))
         def _():
             for i in range(planes):
@@ -105,9 +107,10 @@
 
     def finish(t):
         column_stage(t)
+        outside()
         weight_stage(t)
 
-    return (row_stage, finish)
+    return (row_stage, finish, column_stage, outside, weight_stage)
 
 
 def spread_kernel(n_omega, n_row, frames, limits, weight, first, second, level, mix, thresholds, x, smooth, wide, outgoing, incoming, limit_sem, load_sem, send_sem, recv_sem, row_send, row_recv):
@@ -224,7 +227,7 @@
         for i in range(planes):
             first[i, t, pl.ds(start + 8, 8), :] = p[i] + p[i + 1]
 
-    row_stage, finish = stages(n_row, first, second, smooth, wide, level, mix, weight)
+    row_stage, finish = stages(n_row, first, second, smooth, wide, level, mix, weight)[0:2]
 
     issue(0)
     for t in range(tiles):
@@ -356,15 +359,16 @@
 
     for t in range(tiles - 2):
         store(t).start()
-    row_stage, finish = stages(n_row, first, second, smooth, wide, level, mix, weight)
+    row_stage = stages(n_row, first, second, smooth.at[0], wide.at[0], level, mix, weight)[0]
     row_stage(tiles - 1)
 
-    def tail(t, carry):
-        finish(t)
-        store(t).start()
-        return carry
-
-    lax.fori_loop(tiles - 2, tiles, tail, 0)
+    ends = [stages(n_row, first, second, smooth.at[j], wide.at[j], level, mix, weight)[2:] for j in range(2)]
+    for j in range(2):
+        ends[j][0](tiles - 2 + j)
+    for j in range(2):
+        ends[j][1]()
+        ends[j][2](tiles - 2 + j)
+        store(tiles - 2 + j).start()
     frame_base = lax.axis_index("omega") * depth
     row_base = lax.axis_index("row") * rows
     sub = lax.broadcasted_iota(jnp.int32, (8, LANES), 0)
@@ -466,8 +470,8 @@
         in_specs=[smem(), vmem(), vmem(), vmem(), vmem(), vmem()],
         out_specs=(anywhere(), vmem(), vmem(), vmem()),
         scratch_shapes=[
-            pltpu.VMEM((tall, LANES), jnp.float32),
-            pltpu.VMEM((tall, LANES), jnp.float32),
+            pltpu.VMEM((2, tall, LANES), jnp.float32),
+            pltpu.VMEM((2, tall, LANES), jnp.float32),
             pltpu.VMEM((4, slots * 8, LANES), jnp.float32),
             pltpu.SemaphoreType.DMA((tiles,)),
         ],

time: 53.7 us -> 54 us (level)
  no operation moved by 1% of the time
where the time goes in v6:
time: 54 us; the launch traced here: 53.9 us
  Pallas kernels  53.2 us (99%)
  between operations  0.65 us (1%)
    pallas_call x1, Pallas kernels, on_device(): pl.pallas_call(functools.partial(spread_kernel, n_omega, n_row), out_shap...  48.8 us
    pallas_call x1, Pallas kernels, on_device(): pl.pallas_call(functools.partial(moments_kernel, n_row), out_shape=(jax.S...  4.48 us

profile of v6, /device:TPU:1, one launch (start us, length us, event | category | flops | bytes accessed | tf_op | source)
XLA Modules:
  0.0 53.9 jit_solution(12911831023921554483)
XLA Ops:
  0.6 0.0 copy-start
  0.6 48.8 %spread.1 = (f32[16,8,64,128]{3,2,1,0:T(8,128)S(1)}, f32[18,8,80,128]{3,2,1,0:T(8,128)S(1)}, f32[10,1296,128]{2,1,0:T(8,128)S(1)}, f32[64,128]{1,0:T(8,128)S(1)}, bf16[256,256]{1,0:T(8,128)(2,1)S(1)}) custom-call(f32[16,64,1024]{2,1,0:T(8,128)} %frames.1, s32[64]{0:T(128)} %limits.1), custom_call_target="tpu_custom_call" | custom-call | tf_op jit(solution)/shard_map/spread/pallas_call | solution.py:445
  49.4 0.0 copy-done
  49.4 4.5 %moments.1 = (f32[16,64,1024]{2,1,0:T(8,128)}, f32[4,32]{1,0:T(4,128)}, f32[10,1296,128]{2,1,0:T(8,128)S(1)}, f32[16,8,64,128]{3,2,1,0:T(8,128)S(1)}) custom-call(s32[3,32]{1,0:T(4,128)S(1)} %copy-done, f32[18,8,80,128]{3,2,1,0:T(8,128)S(1)} %get-tuple-element.9.first, ...), custom_call_target="tpu_custom_call", output_to_operand_aliasing={{2}: (2, {}), {3}: (5, {})} | custom-call | tf_op jit(solution)/shard_map/moments/pallas_call | solution.py:467
Async XLA Ops:
  0.6 48.8 %copy-start = (s32[3,32]{1,0:T(4,128)S(1)}, s32[3,32]{1,0:T(4,128)}, u32[]{:S(2)}) copy-start(s32[3,32]{1,0:T(4,128)} %boxes.1) | copy-start | bytes 1156
